TPU v7x, 128 devices: a whole 4x4x4 slice. The times are simulated.
128 devices in a mesh: lon: 16 (over x_lo, z, core), lat: 8 (over y, x_hi).
Axes of the slice: x: 4 (x_hi: 2, x_lo: 2; x = x_hi * 2 + x_lo), y: 4, z: 4, core: 2. Of those that a mesh axis runs over, the one named last changes fastest.
Arguments:
- height: float32 [1, 1152, 4096], P(None, 'lat', 'lon'), may hold values from -6 to 6
- response: float32 [640], replicated, may hold values from 0.25 to 4
Outputs:
- loading: float32 [1, 1152, 4096], P(None, 'lat', 'lon')
All inputs are finite; a program needn't handle non-finite values.
Results may differ from a plain program's by a relative error of at most 0.00085.
Values sent between devices are 32-bit elements; how exact they have to be, the bound alone decides.
No kernel may reach another device: no remote copies, remote signals or barrier semaphores. Data moves between devices by JAX's collectives and lax.ppermute only.
A program may use at most 64 MiB of HBM per device.

v0:
```python
import jax
import jax.numpy as jnp
from jax import lax
from jax.sharding import PartitionSpec as P

NLAT = 1152
NLON = 4096
MODES = 640


block_degrees = 64
rescale_every = 8
highest = lax.Precision.HIGHEST


def in_blocks(x, dim, devices):
    shape = x.shape
    blocks = x.reshape(*shape[:dim], devices, shape[dim] // devices, *shape[dim + 1 :])
    return jnp.moveaxis(blocks, dim, 0)


def sent_and_summed(x, axis, dim):
    blocks = in_blocks(x, dim, lax.axis_size(axis))
    arrived = lax.all_to_all(blocks, axis, split_axis=0, concat_axis=0, tiled=True)
    return arrived.sum(axis=0)


def copy_for_each(x, axis):
    copies = jnp.broadcast_to(x, (lax.axis_size(axis), *x.shape))
    return lax.all_to_all(copies, axis, split_axis=0, concat_axis=0, tiled=True)


def laid_out(blocks, dim):
    blocks = jnp.moveaxis(blocks, 0, dim)
    shape = blocks.shape
    return blocks.reshape(*shape[:dim], shape[dim] * shape[dim + 1], *shape[dim + 2 :])


def gathered_copies(x, axis, dim):
    blocks = copy_for_each(x, axis)
    return laid_out(blocks, dim)


def colatitude_parts(latitudes):
    colatitude = (latitudes.astype(jnp.float32) + 0.5) * (jnp.pi / NLAT)
    sines = jnp.sin(colatitude)
    return (jnp.cos(colatitude), sines, sines * (jnp.pi / NLAT))


def legendre_sweep(cosines, sines, orders, consume, initial):
    order_float = orders.astype(jnp.float32)
    log_start = 0.5 * (
        lax.lgamma(order_float + 1.5)
        - lax.lgamma(order_float + 1.0)
        - lax.lgamma(jnp.full_like(order_float, 1.5))
    ) - 0.5 * jnp.log(4.0 * jnp.pi)
    log_scale = log_start[:, None] + order_float[:, None] * jnp.log(sines)[None, :]
    zero_field = jnp.zeros(log_scale.shape, jnp.float32)

    def one_block(block_index, carried):
        earlier, latest, log_scale, running = carried
        first_degree = (block_index * block_degrees).astype(jnp.int32)
        factor = jnp.exp(log_scale)
        layers = []
        for offset in range(block_degrees):
            degree = first_degree + offset
            started = degree > orders
            starting = degree == orders
            degree_float = degree.astype(jnp.float32)
            lower_float = degree_float - 1.0
            square_gap = jnp.where(
                started, degree_float * degree_float - order_float * order_float, 1.0
            )
            growth = jnp.sqrt(
                jnp.where(started, (4.0 * degree_float * degree_float - 1.0) / square_gap, 0.0)
            )
            damping = jnp.sqrt(
                jnp.where(
                    started,
                    (lower_float * lower_float - order_float * order_float)
                    / jnp.maximum(4.0 * lower_float * lower_float - 1.0, 1.0),
                    0.0,
                )
            )
            current = jnp.where(
                starting[:, None],
                1.0,
                growth[:, None] * (cosines[None, :] * latest - damping[:, None] * earlier),
            )
            layers.append(current * factor)
            earlier, latest = (latest, current)
            if (offset + 1) % rescale_every == 0:
                largest = jnp.maximum(jnp.maximum(jnp.abs(earlier), jnp.abs(latest)), 1.0)
                earlier = earlier / largest
                latest = latest / largest
                log_scale = log_scale + jnp.log(largest)
                factor = jnp.exp(log_scale)
        legendre = jnp.stack(layers)
        return (earlier, latest, log_scale, consume(running, legendre, first_degree))

    carried = (zero_field, zero_field, log_scale, initial)
    carried = lax.fori_loop(0, MODES // block_degrees, one_block, carried)
    return carried[3]


def analyse(spectrum, latitudes, orders):
    cosines, sines, weights = colatitude_parts(latitudes)
    weighted = spectrum * weights

    def consume(coefficients, legendre, first_degree):
        block_terms = jnp.einsum("lmj,mcfj->lmcf", legendre, weighted, precision=highest)
        return lax.dynamic_update_slice_in_dim(coefficients, block_terms, first_degree, 0)

    initial = jnp.zeros((MODES,) + spectrum.shape[:3], jnp.float32)
    return legendre_sweep(cosines, sines, orders, consume, initial)


def synthesise(scaled, latitudes, orders):
    cosines, sines = colatitude_parts(latitudes)[:2]

    def consume(running, legendre, first_degree):
        scaled_block = lax.dynamic_slice_in_dim(scaled, first_degree, block_degrees, 0)
        return running + jnp.einsum("lmj,lmcf->mcfj", legendre, scaled_block, precision=highest)

    initial = jnp.zeros(scaled.shape[1:] + (latitudes.shape[0],), jnp.float32)
    return legendre_sweep(cosines, sines, orders, consume, initial)


def angle_table(wavenumbers, longitudes):
    product = wavenumbers[:, None] * longitudes[None, :] % NLON
    return product.astype(jnp.float32) * (2.0 * jnp.pi / NLON)


def forward_terms(field, wavenumbers, longitudes):
    angles = angle_table(wavenumbers, longitudes)
    spacing = 2.0 * jnp.pi / NLON
    real_part = jnp.einsum("mk,fjk->mfj", jnp.cos(angles) * spacing, field, precision=highest)
    imag_part = -jnp.einsum("mk,fjk->mfj", jnp.sin(angles) * spacing, field, precision=highest)
    return jnp.stack([real_part, imag_part], axis=1)


def inverse_terms(spectral_parts, wavenumbers, longitudes):
    angles = angle_table(wavenumbers, longitudes)
    weight = jnp.where(wavenumbers == 0, 1.0, 2.0)[:, None]
    real_part = jnp.einsum(
        "mk,mfj->fjk", jnp.cos(angles) * weight, spectral_parts[:, 0], precision=highest
    )
    imag_part = jnp.einsum(
        "mk,mfj->fjk", jnp.sin(angles) * weight, spectral_parts[:, 1], precision=highest
    )
    return real_part - imag_part


def shards(height, response):
    fields, band_rows, lon_cells = height.shape
    lon_count = lax.axis_size("lon")
    lat_count = lax.axis_size("lat")
    lon_index = lax.axis_index("lon")
    lat_index = lax.axis_index("lat")
    local_modes = MODES // lon_count
    longitudes = lon_index * lon_cells + jnp.arange(lon_cells, dtype=jnp.int32)
    wavenumbers = jnp.arange(local_modes * lax.axis_size("lon"), dtype=jnp.int32)
    spectrum = sent_and_summed(forward_terms(height, wavenumbers, longitudes), "lon", 0)
    column_modes = local_modes // lat_count
    columns = lax.all_to_all(spectrum, "lat", split_axis=0, concat_axis=3, tiled=True)
    all_latitudes = jnp.arange(NLAT, dtype=jnp.int32)
    column_orders = (
        lon_index * local_modes
        + lat_index * column_modes
        + jnp.arange(column_modes, dtype=jnp.int32)
    )
    coefficients = analyse(columns, all_latitudes, column_orders)
    scaled = coefficients * response[:, None, None, None]
    column_synthesis = synthesise(scaled, all_latitudes, column_orders)
    synthesis = lax.all_to_all(column_synthesis, "lat", split_axis=3, concat_axis=0, tiled=True)
    shard_piece = gathered_copies(synthesis, "lon", 0)
    wavenumbers = jnp.arange(shard_piece.shape[0], dtype=jnp.int32)
    return inverse_terms(shard_piece, wavenumbers, longitudes)


def solution(mesh):
    placed = (P(None, "lat", "lon"), P())
    return jax.shard_map(
        shards, mesh=mesh, in_specs=placed, out_specs=P(None, "lat", "lon"), check_vma=False
    )
```

profile of v0, /device:TPU:1, one launch (start us, length us, event | category | flops | bytes accessed | tf_op | source)
XLA Modules:
  0.0 324.2 jit_solution(3746720195332624760)
XLA Ops:
  0.9 3.2 convolution_negate_fusion
  4.3 3.1 convolution_bitcast_fusion.2
  8.8 7.7 %all-to-all-start = ((f32[16,40,2,1,144]{4,1,3,2,0:T(8,128)}), f32[16,40,2,1,144]{4,1,3,2,0:T(8,128)S(1)}, u32[]{:S(2)}, u32[]{:S(2)}) async-start(f32[16,40,2,1,144]{4,1,3,2,0:T(8,128)} %copy.655), calls=%async_computation | async-start | bytes 2621440 | tf_op jit(solution)/shard_map/all_to_all | solution.py:24
  16.8 18.3 %all-to-all-done = f32[16,40,2,1,144]{4,1,3,2,0:T(8,128)S(1)} async-done(((f32[16,40,2,1,144]{4,1,3,2,0:T(8,128)}), f32[16,40,2,1,144]{4,1,3,2,0:T(8,128)S(1)}, u32[]{:S(2)}, u32[]{:S(2)}) %all-to-all-start) | async-done | bytes 737312 | tf_op jit(solution)/shard_map/all_to_all | solution.py:24
  35.8 6.6 %all-to-all-start.1 = ((f32[40,2,1,144]{3,1,2,0:T(2,128)}), f32[40,2,1,144]{3,1,2,0:T(2,128)S(1)}, u32[]{:S(2)}, u32[]{:S(2)}) async-start(f32[40,2,1,144]{3,1,2,0:T(2,128)} %copy.657), calls=%async_computation.1 | async-start | bytes 163840 | tf_op jit(solution)/shard_map/all_to_all | solution.py:165
  42.5 6.6 %all-to-all-done.1 = f32[40,2,1,144]{3,1,2,0:T(2,128)S(1)} async-done(((f32[40,2,1,144]{3,1,2,0:T(2,128)}), f32[40,2,1,144]{3,1,2,0:T(2,128)S(1)}, u32[]{:S(2)}, u32[]{:S(2)}) %all-to-all-start.1) | async-done | bytes 46112 | tf_op jit(solution)/shard_map/all_to_all | solution.py:165
  49.3 117.3 %while.52 = (s32[]{:T(128)}, f32[5,1152]{1,0:T(8,128)S(1)}, f32[5,1152]{1,0:T(8,128)S(1)}, f32[5,1152]{1,0:T(8,128)S(1)}, f32[640,5,2,1]{0,2,1,3:T(2,128)S(1)}, ...) while((s32[]{:T(128)}, f32[5,1152]{1,0:T(8,128)S(1)}, ...), condition=%wide.region_2.3_spmd.clone.clone.clone.clone, body=%wide.region_1.2_spmd.clone.clone.clone.clone.sunk | while | flops 11932070 | bytes 11638224 | solution.py:102
  52.4 1.5 exponential_multiply_fusion.4
  56.8 2.3 stack.1964
  59.1 1.4 convolution_bitcast_fusion.4
  63.8 1.5 exponential_multiply_fusion.4
  68.2 2.3 stack.1964
  70.5 1.4 convolution_bitcast_fusion.4
  75.8 1.5 exponential_multiply_fusion.4
  80.3 2.3 stack.1964
  82.6 1.4 convolution_bitcast_fusion.4
  87.2 1.5 exponential_multiply_fusion.4
  91.7 2.3 stack.1964
  94.0 1.4 convolution_bitcast_fusion.4
  99.3 1.5 exponential_multiply_fusion.4
  103.8 2.3 stack.1964
  106.0 1.4 convolution_bitcast_fusion.4
  110.7 1.5 exponential_multiply_fusion.4
  115.2 2.3 stack.1964
  117.4 1.4 convolution_bitcast_fusion.4
  122.8 1.5 exponential_multiply_fusion.4
  127.2 2.3 stack.1964
  129.5 1.4 convolution_bitcast_fusion.4
  134.2 1.5 exponential_multiply_fusion.4
  138.6 2.3 stack.1964
  140.9 1.4 convolution_bitcast_fusion.4
  146.3 1.5 exponential_multiply_fusion.4
  150.7 2.3 stack.1964
  153.0 1.4 convolution_bitcast_fusion.4
  157.6 1.5 exponential_multiply_fusion.4
  162.1 2.3 stack.1964
  166.7 106.4 %while.53 = (s32[]{:T(128)}, f32[5,1152]{1,0:T(8,128)S(1)}, f32[5,1152]{1,0:T(8,128)S(1)}, f32[5,1152]{1,0:T(8,128)S(1)}, f32[5,2,1,1152]{3,1,0,2:T(2,128)S(1)},...) while((s32[]{:T(128)}, f32[5,1152]{1,0:T(8,128)S(1)}, ...), condition=%wide.region_4.5_spmd.clone.clone.clone.clone, body=%wide.region_3.4_spmd.clone.clone.clone.clone.sunk | while | flops 11955110 | bytes 11681745 | solution.py:102
  169.9 1.5 exponential_multiply_fusion.5
  174.4 2.3 stack.1966
  180.6 1.5 exponential_multiply_fusion.5
  185.0 2.3 stack.1966
  191.2 1.5 exponential_multiply_fusion.5
  195.6 2.3 stack.1966
  201.8 1.5 exponential_multiply_fusion.5
  206.3 2.3 stack.1966
  212.4 1.5 exponential_multiply_fusion.5
  216.9 2.3 stack.1966
  223.1 1.5 exponential_multiply_fusion.5
  227.5 2.3 stack.1966
  233.7 1.5 exponential_multiply_fusion.5
  238.1 2.3 stack.1966
  244.3 1.5 exponential_multiply_fusion.5
  248.7 2.3 stack.1966
  254.9 1.5 exponential_multiply_fusion.5
  259.4 2.3 stack.1966
  265.5 1.5 exponential_multiply_fusion.5
  270.0 2.3 stack.1966
  274.3 1.6 reshape.6694
  275.9 9.3 %all_to_all.46 = f32[8,1,1440]{2,1,0:T(1,128)S(1)} all-to-all(f32[8,1,1440]{2,1,0:T(1,128)S(1)} %reshape.6694), channel_id=1, replica_groups=mesh['lon'=16,'lat'=8] {'lat'}, dimensions={0} | all-to-all | bytes 92160 | tf_op jit(solution)/shard_map/all_to_all | solution.py:175
  286.5 1.7 reshape.6695
  290.2 7.1 %all-to-all-start.3 = ((f32[16,40,2,1,144]{4,1,2,3,0:T(8,128)}), f32[16,40,2,1,144]{4,1,2,3,0:T(8,128)S(1)}, u32[]{:S(2)}, u32[]{:S(2)}) async-start(f32[16,40,2,1,144]{4,1,2,3,0:T(8,128)} %broadcast_in_dim.4429), calls=%async_computation.3 | async-start | bytes 2621440 | tf_op jit(solution)/shard_map/all_to_all | solution.py:30
  297.3 18.6 %all-to-all-done.3 = f32[16,40,2,1,144]{4,1,2,3,0:T(8,128)S(1)} async-done(((f32[16,40,2,1,144]{4,1,2,3,0:T(8,128)}), f32[16,40,2,1,144]{4,1,2,3,0:T(8,128)S(1)}, u32[]{:S(2)}, u32[]{:S(2)}) %all-to-all-start.3) | async-done | bytes 737312 | tf_op jit(solution)/shard_map/all_to_all | solution.py:30
  316.0 3.6 %fusion.435 = f32[144,256]{1,0:T(8,128)S(1)} fusion(f32[640,2,1,144]{3,0,1,2:T(8,128)S(1)} %bitcast.1891, f32[640]{0:T(1024)S(1)} %fusion.463, s32[256]{0:T(256)S(1)} %iota_add_fusion.2), kind=kOutput, calls=%fused_computation.1122 | convolution fusion | flops 285573120 | bytes 807936 | tf_op jit(solution)/shard_map/mk,mfj->fjk/dot_general | solution.py:145
  319.5 4.3 %fusion.425 = f32[1,144,256]{2,1,0:T(8,128)} fusion(f32[144,256]{1,0:T(8,128)S(1)} %fusion.435, f32[640,2,1,144]{3,0,1,2:T(8,128)S(1)} %bitcast.1892, f32[640]{0:T(1024)S(1)} %fusion.463, s32[256]{0:T(256)S(1)} %iota_add_fusion.2), kind=kOutput, calls=%fused_computation.1106 | convolution fusion | flops 285609984 | bytes 955392 | tf_op jit(solution)/shard_map/mk,mfj->fjk/dot_general | solution.py:148
  (3456 shorter events, 98.8 us)
Async XLA Ops:
  0.0 0.9 copy-start
  8.8 26.3 %all-to-all-start = ((f32[16,40,2,1,144]{4,1,3,2,0:T(8,128)}), f32[16,40,2,1,144]{4,1,3,2,0:T(8,128)S(1)}, u32[]{:S(2)}, u32[]{:S(2)}) async-start(f32[16,40,2,1,144]{4,1,3,2,0:T(8,128)} %copy.655), calls=%async_computation | async-start | bytes 2621440 | tf_op jit(solution)/shard_map/all_to_all | solution.py:24
  35.8 13.3 %all-to-all-start.1 = ((f32[40,2,1,144]{3,1,2,0:T(2,128)}), f32[40,2,1,144]{3,1,2,0:T(2,128)S(1)}, u32[]{:S(2)}, u32[]{:S(2)}) async-start(f32[40,2,1,144]{3,1,2,0:T(2,128)} %copy.657), calls=%async_computation.1 | async-start | bytes 163840 | tf_op jit(solution)/shard_map/all_to_all | solution.py:165
  49.3 117.4 %copy-start.1 = (f32[640]{0:T(1024)S(1)}, f32[640]{0:T(1024)}, u32[]{:S(2)}) copy-start(f32[640]{0:T(1024)} %param.7) | copy-start | bytes 7684
  290.2 25.7 %all-to-all-start.3 = ((f32[16,40,2,1,144]{4,1,2,3,0:T(8,128)}), f32[16,40,2,1,144]{4,1,2,3,0:T(8,128)S(1)}, u32[]{:S(2)}, u32[]{:S(2)}) async-start(f32[16,40,2,1,144]{4,1,2,3,0:T(8,128)} %broadcast_in_dim.4429), calls=%async_computation.3 | async-start | bytes 2621440 | tf_op jit(solution)/shard_map/all_to_all | solution.py:30
where the time goes:
time: 330 us; the launch traced here: 324 us
  local copies, waits for them, and re-layouts  92.9 us (28%)
  other arithmetic  75.1 us (23%)
  loops' own time  44.1 us (13%)
  waiting for transfers between devices  43.5 us (13%)
  matrix products  37.4 us (11%)
  starting transfers between devices  21.4 us (6%)
  blocking collectives  9.27 us (3%)
    another operation x1300, local copies, waits for them, and re-layouts, one_block(): legendre = jnp.stack(layers)  77.4 us
    another operation x2, loops' own time, legendre_sweep(): carried = lax.fori_loop(0, MODES // block_degrees, one_block, carried)  44.1 us
    mul x20, other arithmetic, one_block(): layers.append(current * factor)  30.9 us
    all_to_all x1, waiting for transfers between devices, copy_for_each(): return lax.all_to_all(copies, axis, split_axis=0, concat_axis=0, tiled=True)  18.6 us
    all_to_all x1, waiting for transfers between devices, sent_and_summed(): lax.all_to_all(blocks, axis, split_axis=0, concat_axis=0, tiled=True)  18.3 us
    another operation x180, other arithmetic, one_block(): legendre = jnp.stack(layers)  15.1 us
    dot_general x10, matrix products, consume(): jnp.einsum('lmj,mcfj->lmcf', legendre, weighted, precision=highest)  14.5 us
    sqrt x640, other arithmetic, one_block(): jnp.sqrt(jnp.where(started, (4.0 * degree_float * degree_float - 1.0) / s...  11.8 us
  transfers between devices with their start and end apart: 3, of which 3 were waited for; matrix products, arithmetic and copies ran while one was open for 0% of the time, Pallas kernels for 0%

commit v1 on v0

v1 whole, which is shorter than its diff:
```python
import math

import numpy as np
import jax
import jax.numpy as jnp
from jax import lax
from jax.experimental import pallas as pl
from jax.experimental.pallas import tpu as pltpu
from jax.sharding import PartitionSpec as P

NLAT = 1152
NLON = 4096
MODES = 640
LON = 16
LAT = 8
DEVICES = LON * LAT
BAND = NLAT // LAT
CELLS = NLON // LON
SLOTS = MODES // DEVICES
LANES = 128
REST = BAND - LANES
PIECES = 2 * SLOTS
ROWS = PIECES + 2
HALF = LAT // 2
DEPTH = (HALF + 1) * LANES
STEP = 16
BIG = 2.0**60
SMALL = 2.0**-60

f32 = jnp.float32
bf16 = jnp.bfloat16

SLOT_BASE = [sum(MODES - DEVICES * q for q in range(s)) for s in range(SLOTS)]
LEGENDRE_ROWS = sum(MODES - DEVICES * s for s in range(SLOTS))


def split_np(x):
    x = np.asarray(x, np.float32)
    hi = x.astype(jnp.bfloat16)
    lo = (x - hi.astype(np.float32)).astype(jnp.bfloat16)
    return hi, lo


def wave_table():
    m = np.arange(MODES)[:, None]
    r = np.arange(CELLS)[None, :]
    angle = 2.0 * np.pi * ((m * r) % NLON) / NLON
    parts = np.stack([np.cos(angle), -np.sin(angle)]).reshape(2, SLOTS, DEVICES, CELLS)
    return parts.transpose(1, 0, 2, 3).reshape(2 * MODES, CELLS)


def half_rows(values, fill):
    out = np.full((8, LANES), fill, np.float64)
    for y in range(HALF):
        out[y] = values[BAND * y : BAND * y + LANES]
        out[HALF, REST * y : REST * (y + 1)] = values[BAND * y + LANES : BAND * (y + 1)]
    return out


def row_tables():
    theta = np.pi * (np.arange(NLAT // 2) + 0.5) / NLAT
    cosines = half_rows(np.cos(theta), 0.0)
    logs = half_rows(np.log2(np.sin(theta)), 0.0)
    weights = half_rows(np.sin(theta) * np.pi / NLAT * (2.0 * np.pi / NLON), 0.0)
    coarse = np.round(logs * 4096.0) / 4096.0
    coarse = np.where(np.abs(logs) > 2.0, np.round(logs * 1024.0) / 1024.0, coarse)
    starts = [
        0.5 * (math.lgamma(m + 1.5) - math.lgamma(1.5) - math.lgamma(m + 1.0)) - 0.5 * math.log(4.0 * math.pi)
        for m in range(MODES)
    ]
    starts = np.zeros((8, DEVICES)) + np.pad(np.array(starts).reshape(SLOTS, DEVICES), ((0, 3), (0, 0))) / math.log(2.0)
    return np.stack([cosines, coarse, logs - coarse, weights, starts]).astype(np.float32)


def split(x):
    hi = x.astype(bf16)
    return hi, (x - hi.astype(f32)).astype(bf16)


def dot(a, b):
    return lax.dot_general(a, b, (((1,), (0,)), ((), ())), preferred_element_type=f32)


def dot_nt(a, b):
    return lax.dot_general(a, b, (((1,), (1,)), ((), ())), preferred_element_type=f32)


def iota(shape, dim):
    return lax.broadcasted_iota(jnp.int32, shape, dim)


def ones_where(cond):
    return jnp.where(cond, 1.0, 0.0).astype(bf16)


def phases(lon_index):
    turn = (iota((16, LANES), 0) * lon_index) & 15
    angle = turn.astype(f32) * (2.0 * math.pi / 16)
    return (
        jnp.concatenate([jnp.cos(angle)] * 8, axis=0),
        jnp.concatenate([jnp.sin(angle)] * 8, axis=0),
    )


def forward_kernel(h_ref, whi_ref, wlo_ref, o_ref):
    lon_index = lax.axis_index("lon")
    north = lax.axis_index("lat") < HALF
    hi, lo = split(h_ref[0])
    out_row = iota((2 * LANES, BAND), 0)
    in_row = iota((2 * LANES, BAND), 1)
    order = ones_where(in_row == jnp.where(north, out_row, BAND - 1 - out_row))
    hi = dot(order, hi).astype(bf16)
    lo = dot(order, lo).astype(bf16)
    cos, sin = phases(lon_index)
    rest = [jnp.zeros((DEVICES, LANES), f32), jnp.zeros((DEVICES, LANES), f32)]
    for s in range(SLOTS):
        whi = whi_ref[pl.ds(256 * s, 256), :]
        wlo = wlo_ref[pl.ds(256 * s, 256), :]
        terms = dot_nt(whi, hi) + (dot_nt(wlo, hi) + dot_nt(whi, lo))
        for half in range(2):
            real = terms[:DEVICES, LANES * half : LANES * (half + 1)]
            imag = terms[DEVICES:, LANES * half : LANES * (half + 1)]
            turned = (real * cos + imag * sin, imag * cos - real * sin)
            for c in range(2):
                piece = 2 * s + c
                if half == 0:
                    o_ref[pl.ds(piece, DEVICES, stride=ROWS), :] = turned[c]
                else:
                    shift = REST * (piece % 8)
                    moved = pltpu.roll(turned[c], shift, 1) if shift else turned[c]
                    rest[piece // 8] = rest[piece // 8] + moved
    o_ref[pl.ds(PIECES, DEVICES, stride=ROWS), :] = rest[0]
    o_ref[pl.ds(PIECES + 1, DEVICES, stride=ROWS), :] = rest[1]


def legendre_kernel(coef_ref, tab_ref, phi_ref, plo_ref, stage_ref):
    device = lax.axis_index("lon") * LAT + lax.axis_index("lat")
    x = tab_ref[0]
    coarse = tab_ref[1]
    fine = tab_ref[2]
    lane = iota((1, DEVICES), 1)
    firsts, counts = [], []
    for s in range(SLOTS):
        order = (device + DEVICES * s).astype(f32)
        start = jnp.sum(jnp.where(lane == device, tab_ref[4, pl.ds(s, 1), :], 0.0), axis=1, keepdims=True)
        whole = order * coarse
        count = jnp.maximum(jnp.ceil(-whole * (1.0 / 60.0)), 0.0)
        firsts.append(jnp.exp2((whole + 60.0 * count) + (order * fine + start)))
        counts.append(count)
    zero = jnp.zeros((8, LANES), f32)
    state = [(zero, zero, counts[s]) for s in range(SLOTS)]
    for block in range(SLOTS):
        active = block + 1

        def group(g, carried, block=block, active=active):
            carried = list(carried)
            factors = []
            for s in range(active):
                count = carried[3 * s + 2]
                factors.append(
                    jnp.where(
                        count < 0.5,
                        1.0,
                        jnp.where(count < 1.5, SMALL, jnp.where(count < 2.5, SMALL * SMALL, 0.0)),
                    )
                )
            for n in range(STEP):
                degree = block * DEVICES + g * STEP + n
                for s in range(active):
                    earlier, latest = carried[3 * s], carried[3 * s + 1]
                    growth = coef_ref[s * MODES + degree]
                    damped = coef_ref[(SLOTS + s) * MODES + degree]
                    current = (growth * x) * latest - damped * earlier
                    if s == block:
                        current = jnp.where(degree == device + DEVICES * s, firsts[s], current)
                    row = s * DEVICES * 8 + (g * STEP + n) * 8
                    stage_ref[pl.ds(pl.multiple_of(row, 8), 8), :] = current * factors[s]
                    carried[3 * s], carried[3 * s + 1] = latest, current
            for s in range(active):
                earlier, latest, count = carried[3 * s : 3 * s + 3]
                largest = jnp.maximum(jnp.abs(earlier), jnp.abs(latest))
                large = jnp.logical_and(largest > BIG, count > 0.5)
                scale = jnp.where(large, SMALL, 1.0)
                carried[3 * s] = earlier * scale
                carried[3 * s + 1] = latest * scale
                carried[3 * s + 2] = count - jnp.where(large, 1.0, 0.0)
            return tuple(carried)

        flat = tuple(v for s in range(active) for v in state[s])
        flat = lax.fori_loop(0, DEVICES // STEP, group, flat)
        for s in range(active):
            state[s] = flat[3 * s : 3 * s + 3]
            first = SLOT_BASE[s] + (block - s) * DEVICES
            for b in range(HALF + 1):
                piece = stage_ref[pl.ds(s * DEVICES * 8 + b, DEVICES, stride=8), :]
                hi, lo = split(piece)
                phi_ref[pl.ds(first, DEVICES), LANES * b : LANES * (b + 1)] = hi
                plo_ref[pl.ds(first, DEVICES), LANES * b : LANES * (b + 1)] = lo


def degree_kernel(t_ref, phi_ref, plo_ref, tab_ref, resp_ref, o_ref, sum_ref, fold_ref, rest_ref, back_ref):
    device = lax.axis_index("lon") * LAT + lax.axis_index("lat")
    block = LAT * ROWS
    total = t_ref[pl.ds(0, block), :]
    for i in range(1, LON):
        total = total + t_ref[pl.ds(block * i, block), :]
    sum_ref[...] = total
    fold_ref[...] = jnp.zeros(fold_ref.shape, f32)
    piece = iota((16, LANES), 0)
    own = jnp.logical_and((iota((16, LANES), 1) // REST) == piece % 8, piece < PIECES)
    for y in range(HALF):
        upper = sum_ref[pl.ds(ROWS * y, ROWS), :]
        lower = sum_ref[pl.ds(ROWS * (LAT - 1 - y), ROWS), :]
        for p, folded in enumerate((upper + lower, upper - lower)):
            fold_ref[pl.ds(16 * p, ROWS), LANES * y : LANES * (y + 1)] = folded * tab_ref[3, pl.ds(y, 1), :]
            spread = jnp.where(piece < 8, folded[PIECES : PIECES + 1], folded[PIECES + 1 : PIECES + 2])
            rest_ref[pl.ds(16 * p, 16), LANES * y : LANES * (y + 1)] = jnp.where(own, spread, 0.0)
    lane_in = iota((HALF * LANES, LANES), 0)
    lane_out = iota((HALF * LANES, LANES), 1)
    place = ones_where(
        jnp.logical_and(lane_in % REST == lane_out % REST, lane_in // LANES == lane_out // REST)
    )
    rest_hi, rest_lo = split(rest_ref[...])
    rest = dot(rest_hi, place) + dot(rest_lo, place)
    fold_ref[:, DEPTH - LANES :] = rest * tab_ref[3, pl.ds(HALF, 1), :]
    fold_hi, fold_lo = split(fold_ref[...])
    both = jnp.concatenate([fold_hi, fold_lo], axis=0)
    back_ref[...] = jnp.zeros(back_ref.shape, f32)
    for s in range(SLOTS):
        count = MODES - DEVICES * s
        rows = pl.ds(SLOT_BASE[s], count)
        phi = phi_ref[rows, :]
        plo = plo_ref[rows, :]
        main = dot_nt(both, phi)
        terms = main[:32] + (main[32:] + dot_nt(fold_hi, plo))
        even = ((iota((2, count), 1) + device) & 1) == 0
        chosen = jnp.where(even, terms[2 * s : 2 * s + 2], terms[16 + 2 * s : 18 + 2 * s])
        weight = 2.0 if s else jnp.where(device == 0, 1.0, 2.0)
        scaled = chosen * (resp_ref[:, DEVICES * s :] * weight)
        four = jnp.concatenate(
            [jnp.where(even, scaled, 0.0), jnp.where(even, 0.0, scaled), jnp.zeros((4, count), f32)], axis=0
        )
        hi, lo = split(four)
        pair = jnp.concatenate([hi, lo], axis=0)
        out = dot(pair, phi)
        sums = out[:8] + (out[8:] + dot(hi, plo))
        back_ref[pl.ds(2 * s, 2), :] = sums[0:2] + sums[2:4]
        back_ref[pl.ds(16 + 2 * s, 2), :] = sums[0:2] - sums[2:4]
    pick_in = iota((LANES, HALF * LANES), 0)
    pick_out = iota((LANES, HALF * LANES), 1)
    pick = ones_where(
        jnp.logical_and(pick_in % REST == pick_out % REST, pick_in // REST == pick_out // LANES)
    )
    rest_hi, rest_lo = split(back_ref[:, DEPTH - LANES :])
    rest = dot(rest_hi, pick) + dot(rest_lo, pick)
    for p in range(2):
        for y in range(HALF):
            band = y if p == 0 else LAT - 1 - y
            sum_ref[pl.ds(ROWS * band, PIECES), :] = back_ref[pl.ds(16 * p, PIECES), LANES * y : LANES * (y + 1)]
            kept = jnp.where(own, rest[16 * p : 16 * (p + 1), LANES * y : LANES * (y + 1)], 0.0)
            sum_ref[pl.ds(ROWS * band + PIECES, 1), :] = jnp.sum(kept[:8], axis=0, keepdims=True)
            sum_ref[pl.ds(ROWS * band + PIECES + 1, 1), :] = jnp.sum(kept[8:], axis=0, keepdims=True)
    total = sum_ref[...]
    for i in range(LON):
        o_ref[pl.ds(block * i, block), :] = total


def inverse_kernel(r_ref, whi_ref, wlo_ref, o_ref):
    lon_index = lax.axis_index("lon")
    north = lax.axis_index("lat") < HALF
    cos, sin = phases(lon_index)
    rest = [
        r_ref[pl.ds(PIECES, DEVICES, stride=ROWS), :],
        r_ref[pl.ds(PIECES + 1, DEVICES, stride=ROWS), :],
    ]
    valid = iota((DEVICES, LANES), 1) < REST
    total = None
    for s in range(SLOTS):
        halves = []
        for half in range(2):
            parts = []
            for c in range(2):
                piece = 2 * s + c
                if half == 0:
                    parts.append(r_ref[pl.ds(piece, DEVICES, stride=ROWS), :])
                else:
                    shift = (LANES - REST * (piece % 8)) % LANES
                    moved = pltpu.roll(rest[piece // 8], shift, 1) if shift else rest[piece // 8]
                    parts.append(jnp.where(valid, moved, 0.0))
            real, imag = parts
            halves.append(jnp.concatenate([real * cos - imag * sin, real * sin + imag * cos], axis=0))
        hi, lo = split(jnp.concatenate(halves, axis=1))
        whi = whi_ref[:, 256 * s : 256 * (s + 1)]
        wlo = wlo_ref[:, 256 * s : 256 * (s + 1)]
        terms = dot(whi, hi) + (dot(wlo, hi) + dot(whi, lo))
        total = terms if total is None else total + terms
    out_row = iota((BAND, 2 * LANES), 0)
    in_row = iota((BAND, 2 * LANES), 1)
    order = ones_where(in_row == jnp.where(north, out_row, BAND - 1 - out_row))
    first, rest_of = split(total)
    second, third = split(total - first.astype(f32))
    o_ref[0] = dot_nt(order, first) + (dot_nt(order, second) + dot_nt(order, third))


def vmem(n):
    return [pl.BlockSpec(memory_space=pltpu.VMEM)] * n


def exchanged(x):
    x = x.reshape(DEVICES, 1, ROWS * LANES)
    x = lax.all_to_all(x, ("lon", "lat"), split_axis=0, concat_axis=0, tiled=True)
    return x.reshape(DEVICES * ROWS, LANES)


def recurrence_factors(device):
    degree = jnp.arange(MODES, dtype=jnp.int32)[None, :]
    order = (device + DEVICES * jnp.arange(SLOTS, dtype=jnp.int32))[:, None]
    started = degree > order
    l = degree.astype(f32)
    m = order.astype(f32)
    k = l - 1.0
    growth = jnp.where(started, jnp.sqrt((4.0 * l * l - 1.0) / jnp.where(started, l * l - m * m, 1.0)), 0.0)
    damping = jnp.sqrt(jnp.where(started, k * k - m * m, 0.0) / jnp.maximum(4.0 * k * k - 1.0, 1.0))
    return jnp.stack([growth, growth * damping]).reshape(2 * SLOTS * MODES)


def shards(height, response):
    device = lax.axis_index("lon") * LAT + lax.axis_index("lat")
    table = wave_table()
    whi, wlo = split_np(table)
    thi, tlo = split_np(table.T)
    tables = jnp.asarray(row_tables())
    packed = jax.ShapeDtypeStruct((DEVICES * ROWS, LANES), f32)
    shares = pl.pallas_call(
        forward_kernel, out_shape=packed, in_specs=vmem(3), out_specs=vmem(1)[0], name="forward_dft"
    )(height, jnp.asarray(whi), jnp.asarray(wlo))
    legendre = jax.ShapeDtypeStruct((LEGENDRE_ROWS, DEPTH), bf16)
    phi, plo = pl.pallas_call(
        legendre_kernel,
        out_shape=(legendre, legendre),
        in_specs=[pl.BlockSpec(memory_space=pltpu.SMEM)] + vmem(1),
        out_specs=tuple(vmem(2)),
        scratch_shapes=[pltpu.VMEM((SLOTS * DEVICES * 8, LANES), f32)],
        name="legendre",
    )(recurrence_factors(device), tables)
    arrived = exchanged(shares)
    synthesis = pl.pallas_call(
        degree_kernel,
        out_shape=packed,
        in_specs=vmem(5),
        out_specs=vmem(1)[0],
        scratch_shapes=[
            pltpu.VMEM((LAT * ROWS, LANES), f32),
            pltpu.VMEM((32, DEPTH), f32),
            pltpu.VMEM((32, HALF * LANES), f32),
            pltpu.VMEM((32, DEPTH), f32),
        ],
        name="degrees",
    )(arrived, phi, plo, tables, response.reshape(1, MODES))
    returned = exchanged(synthesis)
    return pl.pallas_call(
        inverse_kernel,
        out_shape=jax.ShapeDtypeStruct((1, BAND, CELLS), f32),
        in_specs=vmem(3),
        out_specs=vmem(1)[0],
        name="inverse_dft",
    )(returned, jnp.asarray(thi), jnp.asarray(tlo))


def solution(mesh):
    placed = (P(None, "lat", "lon"), P())
    return jax.shard_map(
        shards, mesh=mesh, in_specs=placed, out_specs=P(None, "lat", "lon"), check_vma=False
    )
```

time: 330 us -> 63.5 us (0.19); the launches traced: 324 us -> 62.7 us
  local copies, waits for them, and re-layouts: 92.9 us -> 2.08 us
  other arithmetic: 75.1 us -> 0.12 us
  loops' own time: 44.1 us -> 0 us
  matrix products: 37.4 us -> 0 us
  waiting for transfers between devices: 43.5 us -> 6.11 us
  Pallas kernels: 0 us -> 21.3 us
  blocking collectives: 9.27 us -> 21.5 us
  starting transfers between devices: 21.4 us -> 11.5 us
    another operation x1301 -> x0, local copies, waits for them, and re-layouts: 78.6 us -> none  [the longest x1300 77.4 us: one_block(): legendre = jnp.stack(layers)]
    another operation x2 -> x0, loops' own time: 44.1 us -> none  [legendre_sweep(): carried = lax.fori_loop(0, MODES // block_degrees, one_block, carried)]
    all_to_all x3 -> x1, waiting for transfers between devices: 43.5 us -> 6.11 us  [exchanged(): lax.all_to_all(x, ('lon', 'lat'), split_axis=0, concat_axis=0, tiled=True)]
    dot_general x24 -> x0, matrix products: 37.4 us -> none  [the longest x10 14.5 us: consume(): jnp.einsum('lmj,mcfj->lmcf', legendre, weighted, precision=highest)]
    mul x24 -> x2, other arithmetic: 31 us -> 0.01 us  [the longest x1 0.01 us: recurrence_factors(): m * m]
    sqrt x1280 -> x0, other arithmetic: 21.6 us -> none  [the longest x640 11.8 us: one_block(): jnp.sqrt(jnp.where(started, (4.0 * degree_float * degree_float - 1.0) / s...]
    pallas_call x0 -> x4, Pallas kernels: none -> 21.3 us  [the longest x1 7.76 us: shards(): pl.pallas_call(legendre_kernel, out_shape=(legendre, legendre), in_specs=...]
    another operation x181 -> x1, other arithmetic: 15.2 us -> 0.01 us  [recurrence_factors(): return jnp.stack([growth, growth * damping]).reshape(2 * SLOTS * MODES)]
  transfers between devices with their start and end apart: 3 -> 1, of which waited for: 3 -> 1; matrix products, arithmetic and copies ran while one was open for 0% -> 2% of each run, Pallas kernels for 0% -> 12%
where the time goes in v1:
time: 63.5 us; the launch traced here: 62.7 us
  blocking collectives  21.5 us (34%)
  Pallas kernels  21.3 us (34%)
  starting transfers between devices  11.5 us (18%)
  waiting for transfers between devices  6.11 us (10%)
  local copies, waits for them, and re-layouts  2.08 us (3%)
    all_to_all x1, blocking collectives, exchanged(): lax.all_to_all(x, ('lon', 'lat'), split_axis=0, concat_axis=0, tiled=True)  21.5 us
    all_to_all x1, starting transfers between devices, exchanged(): lax.all_to_all(x, ('lon', 'lat'), split_axis=0, concat_axis=0, tiled=True)  11.5 us
    pallas_call x1, Pallas kernels, shards(): pl.pallas_call(legendre_kernel, out_shape=(legendre, legendre), in_specs=...  7.76 us
    pallas_call x1, Pallas kernels, shards(): pl.pallas_call(degree_kernel, out_shape=packed, in_specs=vmem(5), out_spe...  7.02 us
    all_to_all x1, waiting for transfers between devices, exchanged(): lax.all_to_all(x, ('lon', 'lat'), split_axis=0, concat_axis=0, tiled=True)  6.11 us
    pallas_call x1, Pallas kernels, shards(): pl.pallas_call(inverse_kernel, out_shape=jax.ShapeDtypeStruct((1, BAND, C...  3.36 us
    pallas_call x1, Pallas kernels, shards(): pl.pallas_call(forward_kernel, out_shape=packed, in_specs=vmem(3), out_sp...  3.19 us
  transfers between devices with their start and end apart: 1, of which 1 were waited for; matrix products, arithmetic and copies ran while one was open for 2% of the time, Pallas kernels for 12%

profile of v1, /device:TPU:1, one launch (start us, length us, event | category | flops | bytes accessed | tf_op | source)
XLA Modules:
  0.0 62.7 jit_solution(2134344296615492477)
XLA Ops:
  0.0 0.0 copy-start.1
  0.0 3.2 %forward_dft.1 = f32[1536,128]{1,0:T(8,128)} custom-call(f32[1,144,256]{2,1,0:T(8,128)} %h_ref.1, bf16[1280,256]{1,0:T(8,128)(2,1)} %constant.35.clone.whi_ref, bf16[1280,256]{1,0:T(8,128)(2,1)} %constant.36.clone.wlo_ref), custom_call_target="tpu_custom_call" | custom-call | tf_op jit(solution)/shard_map/forward_dft/pallas_call | solution.py:334
  3.2 11.5 %all-to-all-start = ((f32[128,1,1536]{2,1,0:T(1,128)}), f32[128,1,1536]{2,1,0:T(1,128)S(1)}, u32[]{:S(2)}, u32[]{:S(2)}) async-start(f32[128,1,1536]{2,1,0:T(1,128)} %bitcast.4), calls=%async_computation | async-start | bytes 1572864 | tf_op jit(solution)/shard_map/all_to_all | solution.py:311
  14.7 0.0 copy-done.1
  14.7 0.6 reshape.325.resp_ref
  15.3 0.1 sqrt_select_fusion
  15.4 0.6 reshape.324.coef_ref
  16.0 7.8 %legendre.1 = (bf16[1920,640]{1,0:T(8,128)(2,1)}, bf16[1920,640]{1,0:T(8,128)(2,1)}) custom-call(f32[6400]{0:T(1024)} %reshape.324.coef_ref, f32[5,8,128]{2,1,0:T(8,128)} %constant.34.clone.tab_ref), custom_call_target="tpu_custom_call" | custom-call | tf_op jit(solution)/shard_map/legendre/pallas_call | solution.py:338
  23.8 6.1 %all-to-all-done = f32[128,1,1536]{2,1,0:T(1,128)S(1)} async-done(((f32[128,1,1536]{2,1,0:T(1,128)}), f32[128,1,1536]{2,1,0:T(1,128)S(1)}, u32[]{:S(2)}, u32[]{:S(2)}) %all-to-all-start) | async-done | bytes 786464 | tf_op jit(solution)/shard_map/all_to_all | solution.py:311
  29.9 0.0 copy-start
  29.9 0.9 %copy-done = f32[128,1,1536]{2,1,0:T(1,128)} copy-done((f32[128,1,1536]{2,1,0:T(1,128)}, f32[128,1,1536]{2,1,0:T(1,128)S(1)}, u32[]{:S(2)}) %copy-start) | copy-done | bytes 786456
  30.8 7.0 %degrees.1 = f32[1536,128]{1,0:T(8,128)} custom-call(f32[1536,128]{1,0:T(8,128)} %bitcast.6, bf16[1920,640]{1,0:T(8,128)(2,1)} %get-tuple-element.7.phi_ref, bf16[1920,640]{1,0:T(8,128)(2,1)} %get-tuple-element.8.plo_ref, f32[5,8,128]{2,1,0:T(8,128)} %constant.34.clone.tab_ref, f32[1,640]{1,0:T(1,128)} %reshape.325.resp_ref), custom_call_target="tpu_custom_call" | custom-call | tf_op jit(solution)/shard_map/degrees/pallas_call | solution.py:347
  37.8 21.5 %all_to_all.10 = f32[128,1,1536]{2,1,0:T(1,128)} all-to-all(f32[128,1,1536]{2,1,0:T(1,128)} %bitcast.7), channel_id=1, replica_groups=mesh['lon'=16,'lat'=8] {'lon','lat'}, dimensions={0} | all-to-all | bytes 1572864 | tf_op jit(solution)/shard_map/all_to_all | solution.py:311
  59.3 3.4 %inverse_dft.1 = f32[1,144,256]{2,1,0:T(8,128)} custom-call(f32[1536,128]{1,0:T(8,128)} %bitcast.5, bf16[256,1280]{1,0:T(8,128)(2,1)} %constant.37.clone.whi_ref, bf16[256,1280]{1,0:T(8,128)(2,1)} %constant.38.clone.wlo_ref), custom_call_target="tpu_custom_call" | custom-call | tf_op jit(solution)/shard_map/inverse_dft/pallas_call | solution.py:361
  (5 shorter events, 0.0 us)
Async XLA Ops:
  0.0 14.7 %copy-start.1 = (f32[640]{0:T(1024)S(1)}, f32[640]{0:T(1024)}, u32[]{:S(2)}) copy-start(f32[640]{0:T(1024)} %param.8) | copy-start | bytes 7684
  3.2 26.7 %all-to-all-start = ((f32[128,1,1536]{2,1,0:T(1,128)}), f32[128,1,1536]{2,1,0:T(1,128)S(1)}, u32[]{:S(2)}, u32[]{:S(2)}) async-start(f32[128,1,1536]{2,1,0:T(1,128)} %bitcast.4), calls=%async_computation | async-start | bytes 1572864 | tf_op jit(solution)/shard_map/all_to_all | solution.py:311
  29.9 0.9 %copy-start = (f32[128,1,1536]{2,1,0:T(1,128)}, f32[128,1,1536]{2,1,0:T(1,128)S(1)}, u32[]{:S(2)}) copy-start(f32[128,1,1536]{2,1,0:T(1,128)S(1)} %all-to-all-done) | copy-start | bytes 2359300

commit v2 on v1

--- a/solution.py
+++ b/solution.py
@@ -18,12 +18,15 @@
 CELLS = NLON // LON
 SLOTS = MODES // DEVICES
 LANES = 128
-REST = BAND - LANES
-PIECES = 2 * SLOTS
-ROWS = PIECES + 2
+PART = BAND // 2
+MAIN = 64
+REST = PART - MAIN
+ROWS = SLOTS + 1
+PAIRS = LON // 2
 HALF = LAT // 2
 DEPTH = (HALF + 1) * LANES
 STEP = 16
+LEGENDRE_FIRST = False
 BIG = 2.0**60
 SMALL = 2.0**-60
 
@@ -52,8 +55,11 @@
 def half_rows(values, fill):
     out = np.full((8, LANES), fill, np.float64)
     for y in range(HALF):
-        out[y] = values[BAND * y : BAND * y + LANES]
-        out[HALF, REST * y : REST * (y + 1)] = values[BAND * y + LANES : BAND * (y + 1)]
+        for c in range(2):
+            part = values[BAND * y + PART * c : BAND * y + PART * (c + 1)]
+            out[y, MAIN * c : MAIN * (c + 1)] = part[:MAIN]
+            first = REST * (2 * y + c)
+            out[HALF, first : first + REST] = part[MAIN:]
     return out
 
 
@@ -102,35 +108,44 @@
     )
 
 
-def forward_kernel(h_ref, whi_ref, wlo_ref, o_ref):
+def turned_back(terms, cos, sin):
+    real, imag = terms[:DEVICES], terms[DEVICES:]
+    return real * cos + imag * sin, imag * cos - real * sin
+
+
+def forward_kernel(h_ref, g_ref, whi_ref, wlo_ref, o_ref):
     lon_index = lax.axis_index("lon")
+    part = lon_index & 1
     north = lax.axis_index("lat") < HALF
-    hi, lo = split(h_ref[0])
-    out_row = iota((2 * LANES, BAND), 0)
-    in_row = iota((2 * LANES, BAND), 1)
-    order = ones_where(in_row == jnp.where(north, out_row, BAND - 1 - out_row))
-    hi = dot(order, hi).astype(bf16)
-    lo = dot(order, lo).astype(bf16)
-    cos, sin = phases(lon_index)
-    rest = [jnp.zeros((DEVICES, LANES), f32), jnp.zeros((DEVICES, LANES), f32)]
+    own_hi, own_lo = split(h_ref[0])
+    got_hi, got_lo = split(g_ref[0])
+    out_row = iota((LANES, BAND), 0)
+    place = PART * part + out_row
+    source = jnp.where(north, place, BAND - 1 - place)
+    own = ones_where(jnp.logical_and(iota((LANES, BAND), 1) == source, out_row < PART))
+    out_row = iota((LANES, PART), 0)
+    source = jnp.where(north, out_row, PART - 1 - out_row)
+    got = ones_where(jnp.logical_and(iota((LANES, PART), 1) == source, out_row < PART))
+    hi = jnp.concatenate([dot(own, own_hi), dot(got, got_hi)], axis=0).astype(bf16)
+    lo = jnp.concatenate([dot(own, own_lo), dot(got, got_lo)], axis=0).astype(bf16)
+    own_cos, own_sin = phases(lon_index)
+    got_cos, got_sin = phases(lon_index ^ 1)
+    lane = iota((DEVICES, LANES), 1)
+    is_rest = lane // REST == MAIN // REST
+    rest = jnp.zeros((DEVICES, LANES), f32)
     for s in range(SLOTS):
         whi = whi_ref[pl.ds(256 * s, 256), :]
         wlo = wlo_ref[pl.ds(256 * s, 256), :]
         terms = dot_nt(whi, hi) + (dot_nt(wlo, hi) + dot_nt(whi, lo))
-        for half in range(2):
-            real = terms[:DEVICES, LANES * half : LANES * (half + 1)]
-            imag = terms[DEVICES:, LANES * half : LANES * (half + 1)]
-            turned = (real * cos + imag * sin, imag * cos - real * sin)
-            for c in range(2):
-                piece = 2 * s + c
-                if half == 0:
-                    o_ref[pl.ds(piece, DEVICES, stride=ROWS), :] = turned[c]
-                else:
-                    shift = REST * (piece % 8)
-                    moved = pltpu.roll(turned[c], shift, 1) if shift else turned[c]
-                    rest[piece // 8] = rest[piece // 8] + moved
-    o_ref[pl.ds(PIECES, DEVICES, stride=ROWS), :] = rest[0]
-    o_ref[pl.ds(PIECES + 1, DEVICES, stride=ROWS), :] = rest[1]
+        own_real, own_imag = turned_back(terms[:, :LANES], own_cos, own_sin)
+        got_real, got_imag = turned_back(terms[:, LANES:], got_cos, got_sin)
+        real, imag = own_real + got_real, own_imag + got_imag
+        o_ref[pl.ds(s, DEVICES, stride=ROWS), :] = jnp.where(lane < MAIN, real, pltpu.roll(imag, MAIN, 1))
+        for c, value in enumerate((real, imag)):
+            shift = (REST * (s + 8 * c) - MAIN) % LANES
+            kept = jnp.where(is_rest, value, 0.0)
+            rest = rest + (pltpu.roll(kept, shift, 1) if shift else kept)
+    o_ref[pl.ds(SLOTS, DEVICES, stride=ROWS), :] = rest
 
 
 def legendre_kernel(coef_ref, tab_ref, phi_ref, plo_ref, stage_ref):
@@ -201,22 +216,32 @@
 def degree_kernel(t_ref, phi_ref, plo_ref, tab_ref, resp_ref, o_ref, sum_ref, fold_ref, rest_ref, back_ref):
     device = lax.axis_index("lon") * LAT + lax.axis_index("lat")
     block = LAT * ROWS
-    total = t_ref[pl.ds(0, block), :]
-    for i in range(1, LON):
-        total = total + t_ref[pl.ds(block * i, block), :]
-    sum_ref[...] = total
+    for c in range(2):
+        total = t_ref[pl.ds(block * c, block), :]
+        for i in range(1, PAIRS):
+            total = total + t_ref[pl.ds(block * (2 * i + c), block), :]
+        sum_ref[pl.ds(block * c, block), :] = total
     fold_ref[...] = jnp.zeros(fold_ref.shape, f32)
-    piece = iota((16, LANES), 0)
-    own = jnp.logical_and((iota((16, LANES), 1) // REST) == piece % 8, piece < PIECES)
+    own = iota((16, LANES), 1) // REST == iota((16, LANES), 0)
+    first = iota((ROWS, LANES), 1) < MAIN
     for y in range(HALF):
-        upper = sum_ref[pl.ds(ROWS * y, ROWS), :]
-        lower = sum_ref[pl.ds(ROWS * (LAT - 1 - y), ROWS), :]
-        for p, folded in enumerate((upper + lower, upper - lower)):
-            fold_ref[pl.ds(16 * p, ROWS), LANES * y : LANES * (y + 1)] = folded * tab_ref[3, pl.ds(y, 1), :]
-            spread = jnp.where(piece < 8, folded[PIECES : PIECES + 1], folded[PIECES + 1 : PIECES + 2])
-            rest_ref[pl.ds(16 * p, 16), LANES * y : LANES * (y + 1)] = jnp.where(own, spread, 0.0)
-    lane_in = iota((HALF * LANES, LANES), 0)
-    lane_out = iota((HALF * LANES, LANES), 1)
+        mains = []
+        for c in range(2):
+            upper = sum_ref[pl.ds(block * c + ROWS * y, ROWS), :]
+            lower = sum_ref[pl.ds(block * c + ROWS * (LAT - 1 - y), ROWS), :]
+            mains.append((upper + lower, upper - lower))
+        lanes = slice(LANES * y, LANES * (y + 1))
+        for p in range(2):
+            left, right = mains[0][p], mains[1][p]
+            weight = tab_ref[3, pl.ds(y, 1), :]
+            fold_ref[pl.ds(16 * p, ROWS), lanes] = jnp.where(first, left, pltpu.roll(right, MAIN, 1)) * weight
+            fold_ref[pl.ds(16 * p + 8, ROWS), lanes] = jnp.where(first, pltpu.roll(left, MAIN, 1), right) * weight
+            for c in range(2):
+                spread = jnp.where(own, mains[c][p][SLOTS : SLOTS + 1], 0.0)
+                group = 2 * y + c
+                rest_ref[pl.ds(16 * p, 16), LANES * group : LANES * (group + 1)] = spread
+    lane_in = iota((LAT * LANES, LANES), 0)
+    lane_out = iota((LAT * LANES, LANES), 1)
     place = ones_where(
         jnp.logical_and(lane_in % REST == lane_out % REST, lane_in // LANES == lane_out // REST)
     )
@@ -233,21 +258,30 @@
         plo = plo_ref[rows, :]
         main = dot_nt(both, phi)
         terms = main[:32] + (main[32:] + dot_nt(fold_hi, plo))
-        even = ((iota((2, count), 1) + device) & 1) == 0
-        chosen = jnp.where(even, terms[2 * s : 2 * s + 2], terms[16 + 2 * s : 18 + 2 * s])
+        degree = iota((1, count), 1)
+        even = ((degree + device) & 1) == 0
         weight = 2.0 if s else jnp.where(device == 0, 1.0, 2.0)
-        scaled = chosen * (resp_ref[:, DEVICES * s :] * weight)
+        factor = resp_ref[:, DEVICES * s :] * weight
+        real = jnp.where(even, terms[s : s + 1], terms[16 + s : 17 + s]) * factor
+        imag = jnp.where(even, terms[8 + s : 9 + s], terms[24 + s : 25 + s]) * factor
         four = jnp.concatenate(
-            [jnp.where(even, scaled, 0.0), jnp.where(even, 0.0, scaled), jnp.zeros((4, count), f32)], axis=0
+            [
+                jnp.where(even, real, 0.0),
+                jnp.where(even, imag, 0.0),
+                jnp.where(even, 0.0, real),
+                jnp.where(even, 0.0, imag),
+                jnp.zeros((4, count), f32),
+            ],
+            axis=0,
         )
         hi, lo = split(four)
-        pair = jnp.concatenate([hi, lo], axis=0)
-        out = dot(pair, phi)
+        out = dot(jnp.concatenate([hi, lo], axis=0), phi)
         sums = out[:8] + (out[8:] + dot(hi, plo))
-        back_ref[pl.ds(2 * s, 2), :] = sums[0:2] + sums[2:4]
-        back_ref[pl.ds(16 + 2 * s, 2), :] = sums[0:2] - sums[2:4]
-    pick_in = iota((LANES, HALF * LANES), 0)
-    pick_out = iota((LANES, HALF * LANES), 1)
+        for c in range(2):
+            back_ref[pl.ds(8 * c + s, 1), :] = sums[c : c + 1] + sums[2 + c : 3 + c]
+            back_ref[pl.ds(16 + 8 * c + s, 1), :] = sums[c : c + 1] - sums[2 + c : 3 + c]
+    pick_in = iota((LANES, LAT * LANES), 0)
+    pick_out = iota((LANES, LAT * LANES), 1)
     pick = ones_where(
         jnp.logical_and(pick_in % REST == pick_out % REST, pick_in // REST == pick_out // LANES)
     )
@@ -256,37 +290,44 @@
     for p in range(2):
         for y in range(HALF):
             band = y if p == 0 else LAT - 1 - y
-            sum_ref[pl.ds(ROWS * band, PIECES), :] = back_ref[pl.ds(16 * p, PIECES), LANES * y : LANES * (y + 1)]
-            kept = jnp.where(own, rest[16 * p : 16 * (p + 1), LANES * y : LANES * (y + 1)], 0.0)
-            sum_ref[pl.ds(ROWS * band + PIECES, 1), :] = jnp.sum(kept[:8], axis=0, keepdims=True)
-            sum_ref[pl.ds(ROWS * band + PIECES + 1, 1), :] = jnp.sum(kept[8:], axis=0, keepdims=True)
-    total = sum_ref[...]
-    for i in range(LON):
-        o_ref[pl.ds(block * i, block), :] = total
-
-
-def inverse_kernel(r_ref, whi_ref, wlo_ref, o_ref):
+            lanes = slice(LANES * y, LANES * (y + 1))
+            real = back_ref[pl.ds(16 * p, ROWS), lanes]
+            imag = back_ref[pl.ds(16 * p + 8, ROWS), lanes]
+            for c in range(2):
+                row = block * c + ROWS * band
+                if c == 0:
+                    sum_ref[pl.ds(row, ROWS), :] = jnp.where(first, real, pltpu.roll(imag, MAIN, 1))
+                else:
+                    sum_ref[pl.ds(row, ROWS), :] = jnp.where(first, pltpu.roll(real, MAIN, 1), imag)
+                group = 2 * y + c
+                kept = jnp.where(own, rest[16 * p : 16 * (p + 1), LANES * group : LANES * (group + 1)], 0.0)
+                sum_ref[pl.ds(row + SLOTS, 1), :] = jnp.sum(kept, axis=0, keepdims=True)
+    for c in range(2):
+        total = sum_ref[pl.ds(block * c, block), :]
+        for i in range(PAIRS):
+            o_ref[pl.ds(block * (2 * i + c), block), :] = total
+
+
+def inverse_kernel(r_ref, g_ref, whi_ref, wlo_ref, o_ref):
     lon_index = lax.axis_index("lon")
+    part = lon_index & 1
     north = lax.axis_index("lat") < HALF
     cos, sin = phases(lon_index)
-    rest = [
-        r_ref[pl.ds(PIECES, DEVICES, stride=ROWS), :],
-        r_ref[pl.ds(PIECES + 1, DEVICES, stride=ROWS), :],
-    ]
-    valid = iota((DEVICES, LANES), 1) < REST
+    lane = iota((DEVICES, LANES), 1)
+    is_main = lane < MAIN
+    is_rest = lane // REST == MAIN // REST
     total = None
     for s in range(SLOTS):
         halves = []
-        for half in range(2):
+        for ref in (r_ref, g_ref):
+            main = ref[pl.ds(s, DEVICES, stride=ROWS), :]
+            rest = ref[pl.ds(SLOTS, DEVICES, stride=ROWS), :]
             parts = []
             for c in range(2):
-                piece = 2 * s + c
-                if half == 0:
-                    parts.append(r_ref[pl.ds(piece, DEVICES, stride=ROWS), :])
-                else:
-                    shift = (LANES - REST * (piece % 8)) % LANES
-                    moved = pltpu.roll(rest[piece // 8], shift, 1) if shift else rest[piece // 8]
-                    parts.append(jnp.where(valid, moved, 0.0))
+                shift = (MAIN - REST * (s + 8 * c)) % LANES
+                moved = pltpu.roll(rest, shift, 1) if shift else rest
+                body = pltpu.roll(main, MAIN, 1) if c else main
+                parts.append(jnp.where(is_main, body, jnp.where(is_rest, moved, 0.0)))
             real, imag = parts
             halves.append(jnp.concatenate([real * cos - imag * sin, real * sin + imag * cos], axis=0))
         hi, lo = split(jnp.concatenate(halves, axis=1))
@@ -294,9 +335,11 @@
         wlo = wlo_ref[:, 256 * s : 256 * (s + 1)]
         terms = dot(whi, hi) + (dot(wlo, hi) + dot(whi, lo))
         total = terms if total is None else total + terms
-    out_row = iota((BAND, 2 * LANES), 0)
-    in_row = iota((BAND, 2 * LANES), 1)
-    order = ones_where(in_row == jnp.where(north, out_row, BAND - 1 - out_row))
+    row = iota((BAND, 2 * LANES), 0)
+    place = jnp.where(north, row, BAND - 1 - row) - PART * part
+    mine = jnp.logical_and(place >= 0, place < PART)
+    other = jnp.where(place < 0, place + PART, place - PART) + LANES
+    order = ones_where(iota((BAND, 2 * LANES), 1) == jnp.where(mine, place, other))
     first, rest_of = split(total)
     second, third = split(total - first.astype(f32))
     o_ref[0] = dot_nt(order, first) + (dot_nt(order, second) + dot_nt(order, third))
@@ -304,6 +347,14 @@
 
 def vmem(n):
     return [pl.BlockSpec(memory_space=pltpu.VMEM)] * n
+
+
+def limit(mib):
+    return pltpu.CompilerParams(vmem_limit_bytes=mib * 2**20)
+
+
+def swapped(x):
+    return lax.ppermute(x, "lon", [(i, i ^ 1) for i in range(LON)])
 
 
 def exchanged(x):
@@ -331,9 +382,10 @@
     thi, tlo = split_np(table.T)
     tables = jnp.asarray(row_tables())
     packed = jax.ShapeDtypeStruct((DEVICES * ROWS, LANES), f32)
-    shares = pl.pallas_call(
-        forward_kernel, out_shape=packed, in_specs=vmem(3), out_specs=vmem(1)[0], name="forward_dft"
-    )(height, jnp.asarray(whi), jnp.asarray(wlo))
+    north = lax.axis_index("lat") < HALF
+    part = lax.axis_index("lon") & 1
+    start = jnp.where(north, PART * (1 - part), PART * part)
+    got = swapped(lax.dynamic_slice_in_dim(height, start, PART, 1))
     legendre = jax.ShapeDtypeStruct((LEGENDRE_ROWS, DEPTH), bf16)
     phi, plo = pl.pallas_call(
         legendre_kernel,
@@ -341,8 +393,19 @@
         in_specs=[pl.BlockSpec(memory_space=pltpu.SMEM)] + vmem(1),
         out_specs=tuple(vmem(2)),
         scratch_shapes=[pltpu.VMEM((SLOTS * DEVICES * 8, LANES), f32)],
+        compiler_params=limit(16),
         name="legendre",
     )(recurrence_factors(device), tables)
+    if LEGENDRE_FIRST:
+        height, got, phi, plo = lax.optimization_barrier((height, got, phi, plo))
+    shares = pl.pallas_call(
+        forward_kernel,
+        out_shape=packed,
+        in_specs=vmem(4),
+        out_specs=vmem(1)[0],
+        compiler_params=limit(12),
+        name="forward_dft",
+    )(height, got, jnp.asarray(whi), jnp.asarray(wlo))
     arrived = exchanged(shares)
     synthesis = pl.pallas_call(
         degree_kernel,
@@ -350,21 +413,23 @@
         in_specs=vmem(5),
         out_specs=vmem(1)[0],
         scratch_shapes=[
-            pltpu.VMEM((LAT * ROWS, LANES), f32),
+            pltpu.VMEM((2 * LAT * ROWS, LANES), f32),
             pltpu.VMEM((32, DEPTH), f32),
-            pltpu.VMEM((32, HALF * LANES), f32),
+            pltpu.VMEM((32, LAT * LANES), f32),
             pltpu.VMEM((32, DEPTH), f32),
         ],
+        compiler_params=limit(16),
         name="degrees",
     )(arrived, phi, plo, tables, response.reshape(1, MODES))
     returned = exchanged(synthesis)
     return pl.pallas_call(
         inverse_kernel,
         out_shape=jax.ShapeDtypeStruct((1, BAND, CELLS), f32),
-        in_specs=vmem(3),
+        in_specs=vmem(4),
         out_specs=vmem(1)[0],
+        compiler_params=limit(12),
         name="inverse_dft",
-    )(returned, jnp.asarray(thi), jnp.asarray(tlo))
+    )(returned, swapped(returned), jnp.asarray(thi), jnp.asarray(tlo))
 
 
 def solution(mesh):

time: 63.5 us -> 57.3 us (0.902)
  Pallas kernels: 21.3 us -> 12.7 us
  local copies, waits for them, and re-layouts: 2.08 us -> 7.18 us
  blocking collectives: 21.5 us -> 16.7 us
  starting transfers between devices: 11.5 us -> 13.4 us
    unnamed x4 -> x18, local copies, waits for them, and re-layouts: 0.9 us -> 6.26 us
    all_to_all x1, blocking collectives: 21.5 us -> 16.7 us  [exchanged(): lax.all_to_all(x, ('lon', 'lat'), split_axis=0, concat_axis=0, tiled=True)]
    pallas_call x1, Pallas kernels: 7.02 us -> 3.52 us  [shards(): pl.pallas_call(degree_kernel, out_shape=packed, in_specs=vmem(5), out_spe...]
    ppermute x0 -> x2, starting transfers between devices: none -> 2.96 us  [swapped(): return lax.ppermute(x, 'lon', [(i, i ^ 1) for i in range(LON)])]
    pallas_call x1, Pallas kernels: 7.76 us -> 5.45 us  [shards(): pl.pallas_call(legendre_kernel, out_shape=(legendre, legendre), in_specs=...]
    ppermute x0 -> x2, waiting for transfers between devices: none -> 2.23 us  [swapped(): return lax.ppermute(x, 'lon', [(i, i ^ 1) for i in range(LON)])]
    all_to_all x1, waiting for transfers between devices: 6.11 us -> 4.47 us  [exchanged(): lax.all_to_all(x, ('lon', 'lat'), split_axis=0, concat_axis=0, tiled=True)]
    pallas_call x1, Pallas kernels: 3.36 us -> 1.93 us  [shards(): pl.pallas_call(inverse_kernel, out_shape=jax.ShapeDtypeStruct((1, BAND, C...]
  transfers between devices with their start and end apart: 1 -> 3, of which waited for: 1 -> 3; matrix products, arithmetic and copies ran while one was open for 2% -> 0% of each run, Pallas kernels for 12% -> 10%
where the time goes in v2:
time: 57.3 us; the launch traced here: 56.9 us
  blocking collectives  16.7 us (29%)
  starting transfers between devices  13.4 us (23%)
  Pallas kernels  12.7 us (22%)
  local copies, waits for them, and re-layouts  7.18 us (13%)
  waiting for transfers between devices  6.7 us (12%)
    all_to_all x1, blocking collectives, exchanged(): lax.all_to_all(x, ('lon', 'lat'), split_axis=0, concat_axis=0, tiled=True)  16.7 us
    all_to_all x1, starting transfers between devices, exchanged(): lax.all_to_all(x, ('lon', 'lat'), split_axis=0, concat_axis=0, tiled=True)  10.5 us
    unnamed x18, local copies, waits for them, and re-layouts  6.26 us
    pallas_call x1, Pallas kernels, shards(): pl.pallas_call(legendre_kernel, out_shape=(legendre, legendre), in_specs=...  5.45 us
    all_to_all x1, waiting for transfers between devices, exchanged(): lax.all_to_all(x, ('lon', 'lat'), split_axis=0, concat_axis=0, tiled=True)  4.47 us
    pallas_call x1, Pallas kernels, shards(): pl.pallas_call(degree_kernel, out_shape=packed, in_specs=vmem(5), out_spe...  3.52 us
    ppermute x2, starting transfers between devices, swapped(): return lax.ppermute(x, 'lon', [(i, i ^ 1) for i in range(LON)])  2.96 us
    ppermute x2, waiting for transfers between devices, swapped(): return lax.ppermute(x, 'lon', [(i, i ^ 1) for i in range(LON)])  2.23 us
  transfers between devices with their start and end apart: 3, of which 3 were waited for; matrix products, arithmetic and copies ran while one was open for 0% of the time, Pallas kernels for 10%

profile of v2, /device:TPU:1, one launch (start us, length us, event | category | flops | bytes accessed | tf_op | source)
XLA Modules:
  0.0 56.9 jit_solution(289087006667044672)
XLA Ops:
  0.0 0.0 copy-start.7
  0.0 0.0 copy-start.8
  0.0 0.9 %constant_dynamic-slice_fusion = f32[1,72,256]{2,1,0:T(8,128)S(1)} fusion(f32[1,144,256]{2,1,0:T(8,128)} %h_ref.1, s32[]{:T(128)S(6)} %select_n.47), kind=kLoop, calls=%fused_computation.14 | loop fusion | bytes 147460 | tf_op jit(solution)/shard_map/dynamic_slice | solution.py:388
  0.9 1.4 %collective-permute-start = (f32[1,72,256]{2,1,0:T(8,128)S(1)}, f32[1,72,256]{2,1,0:T(8,128)S(1)}, u32[]{:S(2)}, u32[]{:S(2)}) collective-permute-start(f32[1,72,256]{2,1,0:T(8,128)S(1)} %constant_dynamic-slice_fusion), channel_id=1, source_target_pairs={{0,8},{8,0},{16,24},{24,16},{32,40},{40,32},{48,56},{56,48},{64,72... | collective-permute-start | bytes 221192 | tf_op jit(solution)/shard_map/ppermute | solution.py:357
  2.3 0.9 %collective-permute-done.g_ref = f32[1,72,256]{2,1,0:T(8,128)S(1)} collective-permute-done((f32[1,72,256]{2,1,0:T(8,128)S(1)}, f32[1,72,256]{2,1,0:T(8,128)S(1)}, u32[]{:S(2)}, u32[]{:S(2)}) %collective-permute-start) | collective-permute-done | bytes 73760 | tf_op jit(solution)/shard_map/ppermute | solution.py:357
  3.2 0.0 copy-start.4
  3.2 1.1 %copy-done.4 = bf16[1280,256]{1,0:T(8,128)(2,1)S(1)} copy-done((bf16[1280,256]{1,0:T(8,128)(2,1)S(1)}, bf16[1280,256]{1,0:T(8,128)(2,1)}, u32[]{:S(2)}) %copy-start.4) | copy-done | bytes 655384
  4.3 0.0 copy-start.5
  4.3 1.1 %copy-done.5 = bf16[1280,256]{1,0:T(8,128)(2,1)S(1)} copy-done((bf16[1280,256]{1,0:T(8,128)(2,1)S(1)}, bf16[1280,256]{1,0:T(8,128)(2,1)}, u32[]{:S(2)}) %copy-start.5) | copy-done | bytes 655384
  5.4 0.0 copy-start.6
  5.4 0.9 %copy-done.6 = f32[1,144,256]{2,1,0:T(8,128)S(1)} copy-done((f32[1,144,256]{2,1,0:T(8,128)S(1)}, f32[1,144,256]{2,1,0:T(8,128)}, u32[]{:S(2)}) %copy-start.6) | copy-done | bytes 147480
  6.3 1.8 %forward_dft.1 = f32[768,128]{1,0:T(8,128)} custom-call(f32[1,144,256]{2,1,0:T(8,128)S(1)} %copy-done.6, f32[1,72,256]{2,1,0:T(8,128)S(1)} %collective-permute-done.g_ref, bf16[1280,256]{1,0:T(8,128)(2,1)S(1)} %copy-done.5, bf16[1280,256]{1,0:T(8,128)(2,1)S(1)} %copy-done.4), custom_call_target="tpu_custom_call" | custom-call | tf_op jit(solution)/shard_map/forward_dft/pallas_call | solution.py:401
  8.1 10.5 %all-to-all-start = ((f32[128,1,768]{2,1,0:T(1,128)}), f32[128,1,768]{2,1,0:T(1,128)S(1)}, u32[]{:S(2)}, u32[]{:S(2)}) async-start(f32[128,1,768]{2,1,0:T(1,128)} %bitcast), calls=%async_computation | async-start | bytes 786432 | tf_op jit(solution)/shard_map/all_to_all | solution.py:362
  18.6 0.0 copy-done.8
  18.6 0.1 sqrt_select_fusion
  18.7 0.0 copy-done.7
  18.8 5.4 %legendre.1 = (bf16[1920,640]{1,0:T(8,128)(2,1)S(1)}, bf16[1920,640]{1,0:T(8,128)(2,1)S(1)}) custom-call(f32[6400]{0:T(1024)S(1)} %reshape.324.coef_ref, f32[5,8,128]{2,1,0:T(8,128)S(1)} %copy-done.7), custom_call_target="tpu_custom_call" | custom-call | tf_op jit(solution)/shard_map/legendre/pallas_call | solution.py:390
  24.2 0.0 copy-start
  24.2 1.5 %copy-done = bf16[1920,640]{1,0:T(8,128)(2,1)} copy-done((bf16[1920,640]{1,0:T(8,128)(2,1)}, bf16[1920,640]{1,0:T(8,128)(2,1)S(1)}, u32[]{:S(2)}) %copy-start) | copy-done | bytes 2457624
  25.7 4.5 %all-to-all-done = f32[128,1,768]{2,1,0:T(1,128)S(1)} async-done(((f32[128,1,768]{2,1,0:T(1,128)}), f32[128,1,768]{2,1,0:T(1,128)S(1)}, u32[]{:S(2)}, u32[]{:S(2)}) %all-to-all-start) | async-done | bytes 393248 | tf_op jit(solution)/shard_map/all_to_all | solution.py:362
  30.2 0.0 copy-start.1
  30.2 1.7 %copy-done.1 = bf16[1920,640]{1,0:T(8,128)(2,1)S(1)} copy-done((bf16[1920,640]{1,0:T(8,128)(2,1)S(1)}, bf16[1920,640]{1,0:T(8,128)(2,1)}, u32[]{:S(2)}) %copy-start.1) | copy-done | bytes 2457624
  31.9 0.0 copy-start.2
  31.9 0.0 copy-start.3
  31.9 3.5 %degrees.1 = f32[768,128]{1,0:T(8,128)S(1)} custom-call(f32[768,128]{1,0:T(8,128)S(1)} %bitcast.4, bf16[1920,640]{1,0:T(8,128)(2,1)S(1)} %get-tuple-element.7.phi_ref, bf16[1920,640]{1,0:T(8,128)(2,1)S(1)} %copy-done.1, f32[5,8,128]{2,1,0:T(8,128)S(1)} %copy-done.7, f32[1,640]{1,0:T(1,128)S(1)} %reshape.325.resp_ref), custom_call_target="tpu_custom_call" | custom-call | tf_op jit(solution)/shard_map/degrees/pallas_call | solution.py:410
  35.4 16.7 %all_to_all.10 = f32[128,1,768]{2,1,0:T(1,128)S(1)} all-to-all(f32[128,1,768]{2,1,0:T(1,128)S(1)} %bitcast.5), channel_id=1, replica_groups=mesh['lon'=16,'lat'=8] {'lon','lat'}, dimensions={0} | all-to-all | bytes 786432 | tf_op jit(solution)/shard_map/all_to_all | solution.py:362
  52.0 1.6 %collective-permute-start.1 = (f32[768,128]{1,0:T(8,128)S(1)}, f32[768,128]{1,0:T(8,128)S(1)}, u32[]{:S(2)}, u32[]{:S(2)}) collective-permute-start(f32[768,128]{1,0:T(8,128)S(1)} %bitcast.6), channel_id=1, source_target_pairs={{0,8},{8,0},{16,24},{24,16},{32,40},{40,32},{48,56},{56,48},{64,72... | collective-permute-start | bytes 1179656 | tf_op jit(solution)/shard_map/ppermute | solution.py:357
  53.6 1.3 %collective-permute-done.1.g_ref = f32[768,128]{1,0:T(8,128)S(1)} collective-permute-done((f32[768,128]{1,0:T(8,128)S(1)}, f32[768,128]{1,0:T(8,128)S(1)}, u32[]{:S(2)}, u32[]{:S(2)}) %collective-permute-start.1) | collective-permute-done | bytes 393248 | tf_op jit(solution)/shard_map/ppermute | solution.py:357
  55.0 0.0 copy-done.2
  55.0 0.0 copy-done.3
  55.0 1.9 %inverse_dft.1 = f32[1,144,256]{2,1,0:T(8,128)} custom-call(f32[768,128]{1,0:T(8,128)S(1)} %bitcast.7, f32[768,128]{1,0:T(8,128)S(1)} %collective-permute-done.1.g_ref, bf16[256,1280]{1,0:T(8,128)(2,1)S(1)} %copy-done.3, bf16[256,1280]{1,0:T(8,128)(2,1)S(1)} %copy-done.2), custom_call_target="tpu_custom_call" | custom-call | tf_op jit(solution)/shard_map/inverse_dft/pallas_call | solution.py:425
  (7 shorter events, 0.0 us)
Async XLA Ops:
  0.0 18.7 %copy-start.7 = (f32[5,8,128]{2,1,0:T(8,128)S(1)}, f32[5,8,128]{2,1,0:T(8,128)}, u32[]{:S(2)}) copy-start(f32[5,8,128]{2,1,0:T(8,128)} %constant.44.clone.tab_ref) | copy-start | bytes 61444
  0.0 18.6 %copy-start.8 = (f32[640]{0:T(1024)S(1)}, f32[640]{0:T(1024)}, u32[]{:S(2)}) copy-start(f32[640]{0:T(1024)} %param.8) | copy-start | bytes 7684
  0.9 2.3 %collective-permute-start = (f32[1,72,256]{2,1,0:T(8,128)S(1)}, f32[1,72,256]{2,1,0:T(8,128)S(1)}, u32[]{:S(2)}, u32[]{:S(2)}) collective-permute-start(f32[1,72,256]{2,1,0:T(8,128)S(1)} %constant_dynamic-slice_fusion), channel_id=1, source_target_pairs={{0,8},{8,0},{16,24},{24,16},{32,40},{40,32},{48,56},{56,48},{64,72... | collective-permute-start | bytes 221192 | tf_op jit(solution)/shard_map/ppermute | solution.py:357
  3.2 1.1 %copy-start.4 = (bf16[1280,256]{1,0:T(8,128)(2,1)S(1)}, bf16[1280,256]{1,0:T(8,128)(2,1)}, u32[]{:S(2)}) copy-start(bf16[1280,256]{1,0:T(8,128)(2,1)} %constant.46.clone.wlo_ref) | copy-start | bytes 1966084
  4.3 1.1 %copy-start.5 = (bf16[1280,256]{1,0:T(8,128)(2,1)S(1)}, bf16[1280,256]{1,0:T(8,128)(2,1)}, u32[]{:S(2)}) copy-start(bf16[1280,256]{1,0:T(8,128)(2,1)} %constant.45.clone.whi_ref) | copy-start | bytes 1966084
  5.4 0.9 %copy-start.6 = (f32[1,144,256]{2,1,0:T(8,128)S(1)}, f32[1,144,256]{2,1,0:T(8,128)}, u32[]{:S(2)}) copy-start(f32[1,144,256]{2,1,0:T(8,128)} %h_ref.1) | copy-start | bytes 442372
  8.1 22.0 %all-to-all-start = ((f32[128,1,768]{2,1,0:T(1,128)}), f32[128,1,768]{2,1,0:T(1,128)S(1)}, u32[]{:S(2)}, u32[]{:S(2)}) async-start(f32[128,1,768]{2,1,0:T(1,128)} %bitcast), calls=%async_computation | async-start | bytes 786432 | tf_op jit(solution)/shard_map/all_to_all | solution.py:362
  24.2 1.5 %copy-start = (bf16[1920,640]{1,0:T(8,128)(2,1)}, bf16[1920,640]{1,0:T(8,128)(2,1)S(1)}, u32[]{:S(2)}) copy-start(bf16[1920,640]{1,0:T(8,128)(2,1)S(1)} %get-tuple-element.8.plo_ref) | copy-start | bytes 7372804
  30.2 1.7 %copy-start.1 = (bf16[1920,640]{1,0:T(8,128)(2,1)S(1)}, bf16[1920,640]{1,0:T(8,128)(2,1)}, u32[]{:S(2)}) copy-start(bf16[1920,640]{1,0:T(8,128)(2,1)} %copy-done) | copy-start | bytes 7372804
  31.9 23.1 %copy-start.2 = (bf16[256,1280]{1,0:T(8,128)(2,1)S(1)}, bf16[256,1280]{1,0:T(8,128)(2,1)}, u32[]{:S(2)}) copy-start(bf16[256,1280]{1,0:T(8,128)(2,1)} %constant.48.clone.wlo_ref) | copy-start | bytes 1966084
  31.9 23.1 %copy-start.3 = (bf16[256,1280]{1,0:T(8,128)(2,1)S(1)}, bf16[256,1280]{1,0:T(8,128)(2,1)}, u32[]{:S(2)}) copy-start(bf16[256,1280]{1,0:T(8,128)(2,1)} %constant.47.clone.whi_ref) | copy-start | bytes 1966084
  52.0 2.9 %collective-permute-start.1 = (f32[768,128]{1,0:T(8,128)S(1)}, f32[768,128]{1,0:T(8,128)S(1)}, u32[]{:S(2)}, u32[]{:S(2)}) collective-permute-start(f32[768,128]{1,0:T(8,128)S(1)} %bitcast.6), channel_id=1, source_target_pairs={{0,8},{8,0},{16,24},{24,16},{32,40},{40,32},{48,56},{56,48},{64,72... | collective-permute-start | bytes 1179656 | tf_op jit(solution)/shard_map/ppermute | solution.py:357

commit v3 on v2

--- a/solution.py
+++ b/solution.py
@@ -26,15 +26,19 @@
 HALF = LAT // 2
 DEPTH = (HALF + 1) * LANES
 STEP = 16
-LEGENDRE_FIRST = False
+TURN = NLON // DEVICES
 BIG = 2.0**60
 SMALL = 2.0**-60
 
 f32 = jnp.float32
 bf16 = jnp.bfloat16
 
-SLOT_BASE = [sum(MODES - DEVICES * q for q in range(s)) for s in range(SLOTS)]
-LEGENDRE_ROWS = sum(MODES - DEVICES * s for s in range(SLOTS))
+KEPT = (0, 2)
+SENT = tuple(s for s in range(SLOTS) if s not in KEPT)
+DEGREES = [MODES - DEVICES * s for s in range(SLOTS)]
+SLOT_BASE = [sum(DEGREES[q] for q in (KEPT if s in KEPT else SENT) if q < s) for s in range(SLOTS)]
+KEPT_ROWS = sum(DEGREES[s] for s in KEPT)
+SENT_ROWS = sum(DEGREES[s] for s in SENT)
 
 
 def split_np(x):
@@ -50,6 +54,19 @@
     angle = 2.0 * np.pi * ((m * r) % NLON) / NLON
     parts = np.stack([np.cos(angle), -np.sin(angle)]).reshape(2, SLOTS, DEVICES, CELLS)
     return parts.transpose(1, 0, 2, 3).reshape(2 * MODES, CELLS)
+
+
+def first_waves(table):
+    turns = 2.0 * np.pi * np.arange(8)[:, None] * np.arange(CELLS)[None, :] / TURN
+    turns = np.stack([np.cos(turns), np.sin(turns)], axis=1).reshape(16, CELLS)
+    return np.concatenate([table[: 2 * DEVICES], turns]).astype(np.float32)
+
+
+def last_waves(table):
+    turns = 2.0 * np.pi * np.arange(SLOTS)[:, None] * np.arange(TURN)[None, :] / TURN
+    turns = np.stack([np.cos(turns), np.sin(turns)], axis=1).reshape(2 * SLOTS * TURN, 1)
+    turns = np.broadcast_to(turns, (2 * SLOTS * TURN, LANES))
+    return table[: 2 * DEVICES].T.astype(np.float32), turns.astype(np.float32)
 
 
 def half_rows(values, fill):
@@ -113,21 +130,47 @@
     return real * cos + imag * sin, imag * cos - real * sin
 
 
-def forward_kernel(h_ref, g_ref, whi_ref, wlo_ref, o_ref):
-    lon_index = lax.axis_index("lon")
-    part = lon_index & 1
+def band_order():
+    part = lax.axis_index("lon") & 1
     north = lax.axis_index("lat") < HALF
-    own_hi, own_lo = split(h_ref[0])
-    got_hi, got_lo = split(g_ref[0])
     out_row = iota((LANES, BAND), 0)
     place = PART * part + out_row
     source = jnp.where(north, place, BAND - 1 - place)
-    own = ones_where(jnp.logical_and(iota((LANES, BAND), 1) == source, out_row < PART))
-    out_row = iota((LANES, PART), 0)
-    source = jnp.where(north, out_row, PART - 1 - out_row)
-    got = ones_where(jnp.logical_and(iota((LANES, PART), 1) == source, out_row < PART))
-    hi = jnp.concatenate([dot(own, own_hi), dot(got, got_hi)], axis=0).astype(bf16)
-    lo = jnp.concatenate([dot(own, own_lo), dot(got, got_lo)], axis=0).astype(bf16)
+    return ones_where(jnp.logical_and(iota((LANES, BAND), 1) == source, out_row < PART))
+
+
+def own_kernel(h_hbm, wave_hbm, hi_ref, lo_ref, whi_ref, wlo_ref, h_ref, wave_ref, sems):
+    copies = (
+        pltpu.make_async_copy(wave_hbm, wave_ref, sems.at[0]),
+        pltpu.make_async_copy(h_hbm, h_ref, sems.at[1]),
+    )
+    for copy in copies:
+        copy.start()
+    copies[0].wait()
+    base_cos = wave_ref[pl.ds(0, DEVICES), :]
+    base_sin = wave_ref[pl.ds(DEVICES, DEVICES), :]
+    for s in range(SLOTS):
+        wave = (base_cos, base_sin)
+        if s:
+            turn_cos = wave_ref[pl.ds(2 * DEVICES + 2 * s, 1), :]
+            turn_sin = wave_ref[pl.ds(2 * DEVICES + 2 * s + 1, 1), :]
+            wave = (base_cos * turn_cos + base_sin * turn_sin, base_sin * turn_cos - base_cos * turn_sin)
+        whi, wlo = split(jnp.concatenate(wave, axis=0))
+        whi_ref[pl.ds(256 * s, 256), :] = whi
+        wlo_ref[pl.ds(256 * s, 256), :] = wlo
+    copies[1].wait()
+    hi, lo = split(h_ref[0])
+    order = band_order()
+    hi_ref[...] = dot(order, hi).astype(bf16)
+    lo_ref[...] = dot(order, lo).astype(bf16)
+
+
+def forward_kernel(g_ref, own_hi_ref, own_lo_ref, whi_ref, wlo_ref, o_ref):
+    lon_index = lax.axis_index("lon")
+    order = band_order()
+    got_hi, got_lo = split(g_ref[0])
+    hi = jnp.concatenate([own_hi_ref[...], dot(order, got_hi).astype(bf16)], axis=0)
+    lo = jnp.concatenate([own_lo_ref[...], dot(order, got_lo).astype(bf16)], axis=0)
     own_cos, own_sin = phases(lon_index)
     got_cos, got_sin = phases(lon_index ^ 1)
     lane = iota((DEVICES, LANES), 1)
@@ -148,7 +191,9 @@
     o_ref[pl.ds(SLOTS, DEVICES, stride=ROWS), :] = rest
 
 
-def legendre_kernel(coef_ref, tab_ref, phi_ref, plo_ref, stage_ref):
+def legendre_kernel(
+    coef_ref, tab_ref, phi_ref, plo_ref, phi_hbm, plo_hbm, phi_far, plo_far, stage_ref, sems
+):
     device = lax.axis_index("lon") * LAT + lax.axis_index("lat")
     x = tab_ref[0]
     coarse = tab_ref[1]
@@ -164,8 +209,9 @@
         counts.append(count)
     zero = jnp.zeros((8, LANES), f32)
     state = [(zero, zero, counts[s]) for s in range(SLOTS)]
+    copies = []
     for block in range(SLOTS):
-        active = block + 1
+        active = SLOTS - block
 
         def group(g, carried, block=block, active=active):
             carried = list(carried)
@@ -180,14 +226,15 @@
                     )
                 )
             for n in range(STEP):
-                degree = block * DEVICES + g * STEP + n
+                after = block * DEVICES + g * STEP + n
                 for s in range(active):
                     earlier, latest = carried[3 * s], carried[3 * s + 1]
+                    degree = DEVICES * s + after
                     growth = coef_ref[s * MODES + degree]
                     damped = coef_ref[(SLOTS + s) * MODES + degree]
                     current = (growth * x) * latest - damped * earlier
-                    if s == block:
-                        current = jnp.where(degree == device + DEVICES * s, firsts[s], current)
+                    if block == 0:
+                        current = jnp.where(after == device, firsts[s], current)
                     row = s * DEVICES * 8 + (g * STEP + n) * 8
                     stage_ref[pl.ds(pl.multiple_of(row, 8), 8), :] = current * factors[s]
                     carried[3 * s], carried[3 * s + 1] = latest, current
@@ -203,17 +250,49 @@
 
         flat = tuple(v for s in range(active) for v in state[s])
         flat = lax.fori_loop(0, DEVICES // STEP, group, flat)
-        for s in range(active):
+        for s in reversed(range(active)):
             state[s] = flat[3 * s : 3 * s + 3]
-            first = SLOT_BASE[s] + (block - s) * DEVICES
+            first = SLOT_BASE[s] + block * DEVICES
+            rows = pl.ds(first, DEVICES)
+            hi_ref, lo_ref = (phi_ref, plo_ref) if s in KEPT else (phi_far, plo_far)
             for b in range(HALF + 1):
                 piece = stage_ref[pl.ds(s * DEVICES * 8 + b, DEVICES, stride=8), :]
                 hi, lo = split(piece)
-                phi_ref[pl.ds(first, DEVICES), LANES * b : LANES * (b + 1)] = hi
-                plo_ref[pl.ds(first, DEVICES), LANES * b : LANES * (b + 1)] = lo
-
-
-def degree_kernel(t_ref, phi_ref, plo_ref, tab_ref, resp_ref, o_ref, sum_ref, fold_ref, rest_ref, back_ref):
+                hi_ref[b, rows, :] = hi
+                lo_ref[b, rows, :] = lo
+            if s in SENT:
+                for c, (near, far) in enumerate(((phi_far, phi_hbm), (plo_far, plo_hbm))):
+                    copy = pltpu.make_async_copy(near.at[:, rows], far.at[:, rows], sems.at[c, block, SENT.index(s)])
+                    copy.start()
+                    copies.append(copy)
+    for copy in copies:
+        copy.wait()
+
+
+def degree_kernel(
+    t_ref,
+    phi_ref,
+    plo_ref,
+    phi_hbm,
+    plo_hbm,
+    tab_ref,
+    resp_ref,
+    o_ref,
+    phi_far,
+    plo_far,
+    sum_ref,
+    fold_ref,
+    rest_ref,
+    back_ref,
+    sems,
+):
+    copies = []
+    for s in SENT:
+        rows = pl.ds(SLOT_BASE[s], DEGREES[s])
+        for c, (far, near) in enumerate(((phi_hbm, phi_far), (plo_hbm, plo_far))):
+            copies.append(pltpu.make_async_copy(far.at[:, rows], near.at[:, rows], sems.at[c, SENT.index(s)]))
+    for copy in copies:
+        copy.start()
     device = lax.axis_index("lon") * LAT + lax.axis_index("lat")
     block = LAT * ROWS
     for c in range(2):
@@ -251,13 +330,23 @@
     fold_hi, fold_lo = split(fold_ref[...])
     both = jnp.concatenate([fold_hi, fold_lo], axis=0)
     back_ref[...] = jnp.zeros(back_ref.shape, f32)
+    tables = [None] * SLOTS
+    spectra = [None] * SLOTS
+    for s in KEPT + SENT:
+        if s == SENT[0]:
+            for copy in copies:
+                copy.wait()
+        rows = pl.ds(SLOT_BASE[s], DEGREES[s])
+        hi_ref, lo_ref = (phi_ref, plo_ref) if s in KEPT else (phi_far, plo_far)
+        phi = jnp.concatenate([hi_ref[b, rows, :] for b in range(HALF + 1)], axis=1)
+        plo = jnp.concatenate([lo_ref[b, rows, :] for b in range(HALF + 1)], axis=1)
+        tables[s] = phi, plo
+        main = dot_nt(both, phi)
+        spectra[s] = main[:32] + (main[32:] + dot_nt(fold_hi, plo))
     for s in range(SLOTS):
-        count = MODES - DEVICES * s
-        rows = pl.ds(SLOT_BASE[s], count)
-        phi = phi_ref[rows, :]
-        plo = plo_ref[rows, :]
-        main = dot_nt(both, phi)
-        terms = main[:32] + (main[32:] + dot_nt(fold_hi, plo))
+        count = DEGREES[s]
+        phi, plo = tables[s]
+        terms = spectra[s]
         degree = iota((1, count), 1)
         even = ((degree + device) & 1) == 0
         weight = 2.0 if s else jnp.where(device == 0, 1.0, 2.0)
@@ -308,33 +397,51 @@
             o_ref[pl.ds(block * (2 * i + c), block), :] = total
 
 
-def inverse_kernel(r_ref, g_ref, whi_ref, wlo_ref, o_ref):
-    lon_index = lax.axis_index("lon")
-    part = lon_index & 1
-    north = lax.axis_index("lat") < HALF
-    cos, sin = phases(lon_index)
+def half_inverse(ref, whi_ref, wlo_ref):
+    cos, sin = phases(lax.axis_index("lon"))
     lane = iota((DEVICES, LANES), 1)
     is_main = lane < MAIN
     is_rest = lane // REST == MAIN // REST
+    rest = ref[pl.ds(SLOTS, DEVICES, stride=ROWS), :]
     total = None
     for s in range(SLOTS):
-        halves = []
-        for ref in (r_ref, g_ref):
-            main = ref[pl.ds(s, DEVICES, stride=ROWS), :]
-            rest = ref[pl.ds(SLOTS, DEVICES, stride=ROWS), :]
-            parts = []
-            for c in range(2):
-                shift = (MAIN - REST * (s + 8 * c)) % LANES
-                moved = pltpu.roll(rest, shift, 1) if shift else rest
-                body = pltpu.roll(main, MAIN, 1) if c else main
-                parts.append(jnp.where(is_main, body, jnp.where(is_rest, moved, 0.0)))
-            real, imag = parts
-            halves.append(jnp.concatenate([real * cos - imag * sin, real * sin + imag * cos], axis=0))
-        hi, lo = split(jnp.concatenate(halves, axis=1))
+        main = ref[pl.ds(s, DEVICES, stride=ROWS), :]
+        parts = []
+        for c in range(2):
+            shift = (MAIN - REST * (s + 8 * c)) % LANES
+            moved = pltpu.roll(rest, shift, 1) if shift else rest
+            body = pltpu.roll(main, MAIN, 1) if c else main
+            parts.append(jnp.where(is_main, body, jnp.where(is_rest, moved, 0.0)))
+        real, imag = parts
+        hi, lo = split(jnp.concatenate([real * cos - imag * sin, real * sin + imag * cos], axis=0))
         whi = whi_ref[:, 256 * s : 256 * (s + 1)]
         wlo = wlo_ref[:, 256 * s : 256 * (s + 1)]
         terms = dot(whi, hi) + (dot(wlo, hi) + dot(whi, lo))
         total = terms if total is None else total + terms
+    return total
+
+
+def own_inverse_kernel(r_ref, base_ref, turn_ref, o_ref, whi_ref, wlo_ref):
+    base_cos = base_ref[:, :DEVICES]
+    base_sin = base_ref[:, DEVICES:]
+    for s in range(SLOTS):
+        wave = (base_cos, base_sin)
+        if s:
+            turn_cos = turn_ref[pl.ds(2 * s * TURN, TURN), :]
+            turn_sin = turn_ref[pl.ds((2 * s + 1) * TURN, TURN), :]
+            turn_cos = jnp.concatenate([turn_cos] * (CELLS // TURN), axis=0)
+            turn_sin = jnp.concatenate([turn_sin] * (CELLS // TURN), axis=0)
+            wave = (base_cos * turn_cos + base_sin * turn_sin, base_sin * turn_cos - base_cos * turn_sin)
+        whi, wlo = split(jnp.concatenate(wave, axis=1))
+        whi_ref[:, 256 * s : 256 * (s + 1)] = whi
+        wlo_ref[:, 256 * s : 256 * (s + 1)] = wlo
+    o_ref[...] = half_inverse(r_ref, whi_ref, wlo_ref)
+
+
+def inverse_kernel(g_ref, own_ref, whi_ref, wlo_ref, o_ref):
+    part = lax.axis_index("lon") & 1
+    north = lax.axis_index("lat") < HALF
+    total = jnp.concatenate([own_ref[...], half_inverse(g_ref, whi_ref, wlo_ref)], axis=1)
     row = iota((BAND, 2 * LANES), 0)
     place = jnp.where(north, row, BAND - 1 - row) - PART * part
     mine = jnp.logical_and(place >= 0, place < PART)
@@ -349,8 +456,16 @@
     return [pl.BlockSpec(memory_space=pltpu.VMEM)] * n
 
 
+def hbm(n):
+    return [pl.BlockSpec(memory_space=pltpu.HBM)] * n
+
+
 def limit(mib):
     return pltpu.CompilerParams(vmem_limit_bytes=mib * 2**20)
+
+
+def in_hbm(x):
+    return pltpu.with_memory_space_constraint(jnp.asarray(x), pltpu.HBM)
 
 
 def swapped(x):
@@ -378,50 +493,77 @@
 def shards(height, response):
     device = lax.axis_index("lon") * LAT + lax.axis_index("lat")
     table = wave_table()
-    whi, wlo = split_np(table)
-    thi, tlo = split_np(table.T)
     tables = jnp.asarray(row_tables())
     packed = jax.ShapeDtypeStruct((DEVICES * ROWS, LANES), f32)
-    north = lax.axis_index("lat") < HALF
-    part = lax.axis_index("lon") & 1
-    start = jnp.where(north, PART * (1 - part), PART * part)
-    got = swapped(lax.dynamic_slice_in_dim(height, start, PART, 1))
-    legendre = jax.ShapeDtypeStruct((LEGENDRE_ROWS, DEPTH), bf16)
-    phi, plo = pl.pallas_call(
+    got = swapped(height)
+    kept = jax.ShapeDtypeStruct((HALF + 1, KEPT_ROWS, LANES), bf16)
+    sent = pltpu.HBM((HALF + 1, SENT_ROWS, LANES), bf16)
+    far = [pltpu.VMEM((HALF + 1, SENT_ROWS, LANES), bf16)] * 2
+    near_hi, near_lo, far_hi, far_lo = pl.pallas_call(
         legendre_kernel,
-        out_shape=(legendre, legendre),
+        out_shape=(kept, kept, sent, sent),
         in_specs=[pl.BlockSpec(memory_space=pltpu.SMEM)] + vmem(1),
-        out_specs=tuple(vmem(2)),
-        scratch_shapes=[pltpu.VMEM((SLOTS * DEVICES * 8, LANES), f32)],
+        out_specs=tuple(vmem(2) + hbm(2)),
+        scratch_shapes=far
+        + [
+            pltpu.VMEM((SLOTS * DEVICES * 8, LANES), f32),
+            pltpu.SemaphoreType.DMA((2, SLOTS, len(SENT))),
+        ],
         compiler_params=limit(16),
         name="legendre",
     )(recurrence_factors(device), tables)
-    if LEGENDRE_FIRST:
-        height, got, phi, plo = lax.optimization_barrier((height, got, phi, plo))
+    operand = jax.ShapeDtypeStruct((LANES, CELLS), bf16)
+    waves = jax.ShapeDtypeStruct((2 * MODES, CELLS), bf16)
+    own_hi, own_lo, whi, wlo = pl.pallas_call(
+        own_kernel,
+        out_shape=(operand, operand, waves, waves),
+        in_specs=hbm(2),
+        out_specs=tuple(vmem(4)),
+        scratch_shapes=[
+            pltpu.VMEM((1, BAND, CELLS), f32),
+            pltpu.VMEM((2 * DEVICES + 16, CELLS), f32),
+            pltpu.SemaphoreType.DMA((2,)),
+        ],
+        compiler_params=limit(12),
+        name="own_half",
+    )(in_hbm(height), in_hbm(first_waves(table)))
     shares = pl.pallas_call(
         forward_kernel,
         out_shape=packed,
-        in_specs=vmem(4),
+        in_specs=vmem(5),
         out_specs=vmem(1)[0],
         compiler_params=limit(12),
         name="forward_dft",
-    )(height, got, jnp.asarray(whi), jnp.asarray(wlo))
+    )(got, own_hi, own_lo, whi, wlo)
     arrived = exchanged(shares)
     synthesis = pl.pallas_call(
         degree_kernel,
         out_shape=packed,
-        in_specs=vmem(5),
+        in_specs=vmem(3) + hbm(2) + vmem(2),
         out_specs=vmem(1)[0],
-        scratch_shapes=[
+        scratch_shapes=far
+        + [
             pltpu.VMEM((2 * LAT * ROWS, LANES), f32),
             pltpu.VMEM((32, DEPTH), f32),
             pltpu.VMEM((32, LAT * LANES), f32),
             pltpu.VMEM((32, DEPTH), f32),
+            pltpu.SemaphoreType.DMA((2, len(SENT))),
         ],
         compiler_params=limit(16),
         name="degrees",
-    )(arrived, phi, plo, tables, response.reshape(1, MODES))
+    )(arrived, near_hi, near_lo, in_hbm(far_hi), in_hbm(far_lo), tables, response.reshape(1, MODES))
     returned = exchanged(synthesis)
+    other = swapped(returned)
+    waves = jax.ShapeDtypeStruct((CELLS, 2 * MODES), bf16)
+    base, turns = last_waves(table)
+    own, thi, tlo = pl.pallas_call(
+        own_inverse_kernel,
+        out_shape=(jax.ShapeDtypeStruct((CELLS, LANES), f32), waves, waves),
+        in_specs=vmem(3),
+        out_specs=tuple(vmem(3)),
+        compiler_params=limit(12),
+        name="own_inverse_dft",
+    )(returned, jnp.asarray(base), jnp.asarray(turns))
     return pl.pallas_call(
         inverse_kernel,
         out_shape=jax.ShapeDtypeStruct((1, BAND, CELLS), f32),
@@ -429,7 +571,7 @@
         out_specs=vmem(1)[0],
         compiler_params=limit(12),
         name="inverse_dft",
-    )(returned, swapped(returned), jnp.asarray(thi), jnp.asarray(tlo))
+    )(other, own, thi, tlo)
 
 
 def solution(mesh):

time: 57.3 us -> 51.2 us (0.89)
  local copies, waits for them, and re-layouts: 7.18 us -> 0.03 us
  Pallas kernels: 12.7 us -> 14.4 us
    unnamed x18 -> x8, local copies, waits for them, and re-layouts: 6.26 us -> 0.02 us
    pallas_call x3 -> x5, Pallas kernels: 10.8 us -> 12.7 us  [the longest x1 5.24 us: shards(): pl.pallas_call(legendre_kernel, out_shape=(kept, kept, sent, sent), in_sp...]
    ppermute x2, waiting for transfers between devices: 2.23 us -> 0.5 us  [swapped(): return lax.ppermute(x, 'lon', [(i, i ^ 1) for i in range(LON)])]
    all_to_all x1, waiting for transfers between devices: 4.47 us -> 6.15 us  [exchanged(): lax.all_to_all(x, ('lon', 'lat'), split_axis=0, concat_axis=0, tiled=True)]
    dynamic_slice x1 -> x0, local copies, waits for them, and re-layouts: 0.91 us -> none  [shards(): got = swapped(lax.dynamic_slice_in_dim(height, start, PART, 1))]
  transfers between devices with their start and end apart: 3 -> 3, of which waited for: 3 -> 2; matrix products, arithmetic and copies ran while one was open for 0% -> 0% of each run, Pallas kernels for 10% -> 15%
where the time goes in v3:
time: 51.2 us; the launch traced here: 51 us
  blocking collectives  16.5 us (32%)
  Pallas kernels  14.4 us (28%)
  starting transfers between devices  13.2 us (26%)
  waiting for transfers between devices  6.65 us (13%)
    all_to_all x1, blocking collectives, exchanged(): lax.all_to_all(x, ('lon', 'lat'), split_axis=0, concat_axis=0, tiled=True)  16.5 us
    all_to_all x1, starting transfers between devices, exchanged(): lax.all_to_all(x, ('lon', 'lat'), split_axis=0, concat_axis=0, tiled=True)  10.2 us
    all_to_all x1, waiting for transfers between devices, exchanged(): lax.all_to_all(x, ('lon', 'lat'), split_axis=0, concat_axis=0, tiled=True)  6.15 us
    pallas_call x1, Pallas kernels, shards(): pl.pallas_call(legendre_kernel, out_shape=(kept, kept, sent, sent), in_sp...  5.24 us
    pallas_call x1, Pallas kernels, shards(): pl.pallas_call(degree_kernel, out_shape=packed, in_specs=vmem(3) + hbm(2)...  3.5 us
    ppermute x2, starting transfers between devices, swapped(): return lax.ppermute(x, 'lon', [(i, i ^ 1) for i in range(LON)])  2.96 us
    pallas_call x1, Pallas kernels, shards(): pl.pallas_call(forward_kernel, out_shape=packed, in_specs=vmem(5), out_sp...  1.73 us
    pallas_call x1, Pallas kernels, shards(): pl.pallas_call(inverse_kernel, out_shape=jax.ShapeDtypeStruct((1, BAND, C...  1.7 us
  transfers between devices with their start and end apart: 3, of which 2 were waited for; matrix products, arithmetic and copies ran while one was open for 0% of the time, Pallas kernels for 15%

profile of v3, /device:TPU:1, one launch (start us, length us, event | category | flops | bytes accessed | tf_op | source)
XLA Modules:
  0.0 51.0 jit_solution(8625690951547093047)
XLA Ops:
  0.0 1.4 %collective-permute-start = (f32[1,144,256]{2,1,0:T(8,128)}, f32[1,144,256]{2,1,0:T(8,128)S(1)}, u32[]{:S(2)}, u32[]{:S(2)}) collective-permute-start(f32[1,144,256]{2,1,0:T(8,128)} %h_hbm.1), channel_id=1, source_target_pairs={{0,8},{8,0},{16,24},{24,16},{32,40},{40,32},{48,56},{56,48},{64,72... | collective-permute-start | bytes 442376 | tf_op jit(solution)/shard_map/ppermute | solution.py:472
  1.4 1.4 %own_half.1 = (bf16[128,256]{1,0:T(8,128)(2,1)S(1)}, bf16[128,256]{1,0:T(8,128)(2,1)S(1)}, bf16[1280,256]{1,0:T(8,128)(2,1)S(1)}, bf16[1280,256]{1,0:T(8,128)(2,1)S(1)}) custom-call(f32[1,144,256]{2,1,0:T(8,128)} %h_hbm.1, f32[272,256]{1,0:T(8,128)} %constant.33.clone.wave_hbm), custom_call_target="tpu_custom_call" | custom-call | tf_op jit(solution)/shard_map/own_half/pallas_call | solution.py:517
  2.9 0.0 collective-permute-done.g_ref
  2.9 0.0 copy-start.3
  2.9 0.0 copy-start.2
  2.9 1.7 %forward_dft.1 = f32[768,128]{1,0:T(8,128)} custom-call(f32[1,144,256]{2,1,0:T(8,128)S(1)} %collective-permute-done.g_ref, bf16[128,256]{1,0:T(8,128)(2,1)S(1)} %get-tuple-element.16.own_hi_ref, bf16[128,256]{1,0:T(8,128)(2,1)S(1)} %get-tuple-element.17.own_lo_ref, bf16[1280,256]{1,0:T(8,128)(2,1)S(1)} %get-tuple-element.18.whi_ref, ...), custom_call_target="tpu_custom_call" | custom-call | tf_op jit(solution)/shard_map/forward_dft/pallas_call | solution.py:530
  4.6 10.2 %all-to-all-start = ((f32[128,1,768]{2,1,0:T(1,128)}), f32[128,1,768]{2,1,0:T(1,128)S(1)}, u32[]{:S(2)}, u32[]{:S(2)}) async-start(f32[128,1,768]{2,1,0:T(1,128)} %bitcast), calls=%async_computation | async-start | bytes 786432 | tf_op jit(solution)/shard_map/all_to_all | solution.py:477
  14.9 0.0 copy-done.3
  14.9 0.1 sqrt_select_fusion
  15.0 0.0 copy-done.2
  15.0 5.2 %legendre.1 = (bf16[5,1024,128]{2,1,0:T(8,128)(2,1)S(1)}, bf16[5,1024,128]{2,1,0:T(8,128)(2,1)S(1)}, bf16[5,896,128]{2,1,0:T(8,128)(2,1)}, bf16[5,896,128]{2,1,0:T(8,128)(2,1)}) custom-call(f32[6400]{0:T(1024)S(1)} %reshape.324.coef_ref, f32[5,8,128]{2,1,0:T(8,128)S(1)} %copy-done.2), custom_call_target="tpu_custom_call" | custom-call | tf_op jit(solution)/shard_map/legendre/pallas_call | solution.py:502
  20.3 6.2 %all-to-all-done = f32[128,1,768]{2,1,0:T(1,128)S(1)} async-done(((f32[128,1,768]{2,1,0:T(1,128)}), f32[128,1,768]{2,1,0:T(1,128)S(1)}, u32[]{:S(2)}, u32[]{:S(2)}) %all-to-all-start) | async-done | bytes 393248 | tf_op jit(solution)/shard_map/all_to_all | solution.py:477
  26.4 0.0 copy-start
  26.4 0.0 copy-start.1
  26.4 3.5 %degrees.1 = f32[768,128]{1,0:T(8,128)S(1)} custom-call(f32[768,128]{1,0:T(8,128)S(1)} %bitcast.4, bf16[5,1024,128]{2,1,0:T(8,128)(2,1)S(1)} %get-tuple-element.20.phi_ref, bf16[5,1024,128]{2,1,0:T(8,128)(2,1)S(1)} %get-tuple-element.21.plo_ref, bf16[5,896,128]{2,1,0:T(8,128)(2,1)} %get-tuple-element.22.phi_hbm, ...), custom_call_target="tpu_custom_call" | custom-call | tf_op jit(solution)/shard_map/degrees/pallas_call | solution.py:539
  29.9 16.5 %all_to_all.10 = f32[128,1,768]{2,1,0:T(1,128)S(1)} all-to-all(f32[128,1,768]{2,1,0:T(1,128)S(1)} %bitcast.7), channel_id=1, replica_groups=mesh['lon'=16,'lat'=8] {'lon','lat'}, dimensions={0} | all-to-all | bytes 786432 | tf_op jit(solution)/shard_map/all_to_all | solution.py:477
  46.4 1.6 %collective-permute-start.1 = (f32[768,128]{1,0:T(8,128)S(1)}, f32[768,128]{1,0:T(8,128)S(1)}, u32[]{:S(2)}, u32[]{:S(2)}) collective-permute-start(f32[768,128]{1,0:T(8,128)S(1)} %bitcast.5), channel_id=1, source_target_pairs={{0,8},{8,0},{16,24},{24,16},{32,40},{40,32},{48,56},{56,48},{64,72... | collective-permute-start | bytes 1179656 | tf_op jit(solution)/shard_map/ppermute | solution.py:472
  48.0 0.0 copy-done
  48.0 0.0 copy-done.1
  48.0 0.8 %own_inverse_dft.1 = (f32[256,128]{1,0:T(8,128)S(1)}, bf16[256,1280]{1,0:T(8,128)(2,1)S(1)}, bf16[256,1280]{1,0:T(8,128)(2,1)S(1)}) custom-call(f32[768,128]{1,0:T(8,128)S(1)} %bitcast.6, f32[256,256]{1,0:T(8,128)S(1)} %copy-done, f32[320,128]{1,0:T(8,128)S(1)} %copy-done.1), custom_call_target="tpu_custom_call" | custom-call | tf_op jit(solution)/shard_map/own_inverse_dft/pallas_call | solution.py:559
  48.8 0.5 collective-permute-done.1.g_ref
  49.3 1.7 %inverse_dft.1 = f32[1,144,256]{2,1,0:T(8,128)} custom-call(f32[768,128]{1,0:T(8,128)S(1)} %collective-permute-done.1.g_ref, f32[256,128]{1,0:T(8,128)S(1)} %get-tuple-element.24.own_ref, bf16[256,1280]{1,0:T(8,128)(2,1)S(1)} %get-tuple-element.25.whi_ref, bf16[256,1280]{1,0:T(8,128)(2,1)S(1)} %get-tuple-element.26.wlo_ref), custom_call_target="tpu_custom_call" | custom-call | tf_op jit(solution)/shard_map/inverse_dft/pallas_call | solution.py:567
  (7 shorter events, 0.0 us)
Async XLA Ops:
  0.0 2.9 %collective-permute-start = (f32[1,144,256]{2,1,0:T(8,128)}, f32[1,144,256]{2,1,0:T(8,128)S(1)}, u32[]{:S(2)}, u32[]{:S(2)}) collective-permute-start(f32[1,144,256]{2,1,0:T(8,128)} %h_hbm.1), channel_id=1, source_target_pairs={{0,8},{8,0},{16,24},{24,16},{32,40},{40,32},{48,56},{56,48},{64,72... | collective-permute-start | bytes 442376 | tf_op jit(solution)/shard_map/ppermute | solution.py:472
  2.9 12.0 %copy-start.3 = (f32[640]{0:T(1024)S(1)}, f32[640]{0:T(1024)}, u32[]{:S(2)}) copy-start(f32[640]{0:T(1024)} %param.7) | copy-start | bytes 7684
  2.9 12.1 %copy-start.2 = (f32[5,8,128]{2,1,0:T(8,128)S(1)}, f32[5,8,128]{2,1,0:T(8,128)}, u32[]{:S(2)}) copy-start(f32[5,8,128]{2,1,0:T(8,128)} %constant.32.clone.tab_ref) | copy-start | bytes 61444
  4.6 21.8 %all-to-all-start = ((f32[128,1,768]{2,1,0:T(1,128)}), f32[128,1,768]{2,1,0:T(1,128)S(1)}, u32[]{:S(2)}, u32[]{:S(2)}) async-start(f32[128,1,768]{2,1,0:T(1,128)} %bitcast), calls=%async_computation | async-start | bytes 786432 | tf_op jit(solution)/shard_map/all_to_all | solution.py:477
  26.4 21.5 %copy-start = (f32[256,256]{1,0:T(8,128)S(1)}, f32[256,256]{1,0:T(8,128)}, u32[]{:S(2)}) copy-start(f32[256,256]{1,0:T(8,128)} %constant.34.clone.base_ref) | copy-start | bytes 786436
  26.4 21.5 %copy-start.1 = (f32[320,128]{1,0:T(8,128)S(1)}, f32[320,128]{1,0:T(8,128)}, u32[]{:S(2)}) copy-start(f32[320,128]{1,0:T(8,128)} %constant.35.clone.turn_ref) | copy-start | bytes 491524
  46.4 2.9 %collective-permute-start.1 = (f32[768,128]{1,0:T(8,128)S(1)}, f32[768,128]{1,0:T(8,128)S(1)}, u32[]{:S(2)}, u32[]{:S(2)}) collective-permute-start(f32[768,128]{1,0:T(8,128)S(1)} %bitcast.5), channel_id=1, source_target_pairs={{0,8},{8,0},{16,24},{24,16},{32,40},{40,32},{48,56},{56,48},{64,72... | collective-permute-start | bytes 1179656 | tf_op jit(solution)/shard_map/ppermute | solution.py:472

commit v4 on v3

--- a/solution.py
+++ b/solution.py
@@ -33,7 +33,7 @@
 f32 = jnp.float32
 bf16 = jnp.bfloat16
 
-KEPT = (0, 2)
+KEPT = (0, 1)
 SENT = tuple(s for s in range(SLOTS) if s not in KEPT)
 DEGREES = [MODES - DEVICES * s for s in range(SLOTS)]
 SLOT_BASE = [sum(DEGREES[q] for q in (KEPT if s in KEPT else SENT) if q < s) for s in range(SLOTS)]
@@ -85,6 +85,7 @@
     cosines = half_rows(np.cos(theta), 0.0)
     logs = half_rows(np.log2(np.sin(theta)), 0.0)
     weights = half_rows(np.sin(theta) * np.pi / NLAT * (2.0 * np.pi / NLON), 0.0)
+    weights[HALF, MAIN:] = weights[HALF, :MAIN]
     coarse = np.round(logs * 4096.0) / 4096.0
     coarse = np.where(np.abs(logs) > 2.0, np.round(logs * 1024.0) / 1024.0, coarse)
     starts = [
@@ -116,13 +117,19 @@
     return jnp.where(cond, 1.0, 0.0).astype(bf16)
 
 
-def phases(lon_index):
+def phase_rows(lon_index):
     turn = (iota((16, LANES), 0) * lon_index) & 15
     angle = turn.astype(f32) * (2.0 * math.pi / 16)
-    return (
-        jnp.concatenate([jnp.cos(angle)] * 8, axis=0),
-        jnp.concatenate([jnp.sin(angle)] * 8, axis=0),
-    )
+    return jnp.cos(angle), jnp.sin(angle)
+
+
+def tiled(rows):
+    return jnp.concatenate([rows] * 8, axis=0)
+
+
+def phases(lon_index):
+    cos, sin = phase_rows(lon_index)
+    return tiled(cos), tiled(sin)
 
 
 def turned_back(terms, cos, sin):
@@ -139,13 +146,20 @@
     return ones_where(jnp.logical_and(iota((LANES, BAND), 1) == source, out_row < PART))
 
 
-def own_kernel(h_hbm, wave_hbm, hi_ref, lo_ref, whi_ref, wlo_ref, h_ref, wave_ref, sems):
+def own_kernel(
+    h_hbm, wave_hbm, hi_ref, lo_ref, whi_ref, wlo_ref, phase_ref, order_ref, h_ref, wave_ref, sems
+):
     copies = (
         pltpu.make_async_copy(wave_hbm, wave_ref, sems.at[0]),
         pltpu.make_async_copy(h_hbm, h_ref, sems.at[1]),
     )
     for copy in copies:
         copy.start()
+    lon_index = lax.axis_index("lon")
+    for n, rows in enumerate(phase_rows(lon_index) + phase_rows(lon_index ^ 1)):
+        phase_ref[n] = rows
+    order = band_order()
+    order_ref[...] = order
     copies[0].wait()
     base_cos = wave_ref[pl.ds(0, DEVICES), :]
     base_sin = wave_ref[pl.ds(DEVICES, DEVICES), :]
@@ -160,26 +174,23 @@
         wlo_ref[pl.ds(256 * s, 256), :] = wlo
     copies[1].wait()
     hi, lo = split(h_ref[0])
-    order = band_order()
     hi_ref[...] = dot(order, hi).astype(bf16)
     lo_ref[...] = dot(order, lo).astype(bf16)
 
 
-def forward_kernel(g_ref, own_hi_ref, own_lo_ref, whi_ref, wlo_ref, o_ref):
-    lon_index = lax.axis_index("lon")
-    order = band_order()
+def forward_kernel(g_ref, own_hi_ref, own_lo_ref, whi_ref, wlo_ref, phase_ref, order_ref, o_ref):
+    order = order_ref[...]
     got_hi, got_lo = split(g_ref[0])
     hi = jnp.concatenate([own_hi_ref[...], dot(order, got_hi).astype(bf16)], axis=0)
     lo = jnp.concatenate([own_lo_ref[...], dot(order, got_lo).astype(bf16)], axis=0)
-    own_cos, own_sin = phases(lon_index)
-    got_cos, got_sin = phases(lon_index ^ 1)
+    own_cos, own_sin, got_cos, got_sin = (tiled(phase_ref[n]) for n in range(4))
     lane = iota((DEVICES, LANES), 1)
     is_rest = lane // REST == MAIN // REST
     rest = jnp.zeros((DEVICES, LANES), f32)
+    waves = jnp.concatenate([whi_ref[...], wlo_ref[...], whi_ref[...]], axis=1)
+    all_terms = dot_nt(waves, jnp.concatenate([hi, hi, lo], axis=1))
     for s in range(SLOTS):
-        whi = whi_ref[pl.ds(256 * s, 256), :]
-        wlo = wlo_ref[pl.ds(256 * s, 256), :]
-        terms = dot_nt(whi, hi) + (dot_nt(wlo, hi) + dot_nt(whi, lo))
+        terms = all_terms[256 * s : 256 * (s + 1)]
         own_real, own_imag = turned_back(terms[:, :LANES], own_cos, own_sin)
         got_real, got_imag = turned_back(terms[:, LANES:], got_cos, got_sin)
         real, imag = own_real + got_real, own_imag + got_imag
@@ -191,21 +202,20 @@
     o_ref[pl.ds(SLOTS, DEVICES, stride=ROWS), :] = rest
 
 
-def legendre_kernel(
-    coef_ref, tab_ref, phi_ref, plo_ref, phi_hbm, plo_hbm, phi_far, plo_far, stage_ref, sems
-):
+def legendre_kernel(coef_ref, tab_ref, near_ref, far_hbm, far_ref, stage_ref, sems):
     device = lax.axis_index("lon") * LAT + lax.axis_index("lat")
     x = tab_ref[0]
     coarse = tab_ref[1]
     fine = tab_ref[2]
     lane = iota((1, DEVICES), 1)
+    used = jnp.logical_or(iota((8, LANES), 0) < HALF, iota((8, LANES), 1) < MAIN)
     firsts, counts = [], []
     for s in range(SLOTS):
         order = (device + DEVICES * s).astype(f32)
         start = jnp.sum(jnp.where(lane == device, tab_ref[4, pl.ds(s, 1), :], 0.0), axis=1, keepdims=True)
         whole = order * coarse
         count = jnp.maximum(jnp.ceil(-whole * (1.0 / 60.0)), 0.0)
-        firsts.append(jnp.exp2((whole + 60.0 * count) + (order * fine + start)))
+        firsts.append(jnp.where(used, jnp.exp2((whole + 60.0 * count) + (order * fine + start)), 0.0))
         counts.append(count)
     zero = jnp.zeros((8, LANES), f32)
     state = [(zero, zero, counts[s]) for s in range(SLOTS)]
@@ -254,32 +264,32 @@
             state[s] = flat[3 * s : 3 * s + 3]
             first = SLOT_BASE[s] + block * DEVICES
             rows = pl.ds(first, DEVICES)
-            hi_ref, lo_ref = (phi_ref, plo_ref) if s in KEPT else (phi_far, plo_far)
+            ref = near_ref if s in KEPT else far_ref
             for b in range(HALF + 1):
-                piece = stage_ref[pl.ds(s * DEVICES * 8 + b, DEVICES, stride=8), :]
-                hi, lo = split(piece)
-                hi_ref[b, rows, :] = hi
-                lo_ref[b, rows, :] = lo
+                hi, lo = split(stage_ref[pl.ds(s * DEVICES * 8 + b, DEVICES, stride=8), :])
+                if b < HALF:
+                    ref[b, rows, :] = hi
+                    ref[HALF + b, rows, :] = lo
+                else:
+                    ref[2 * HALF, rows, :] = (hi.astype(f32) + pltpu.roll(lo.astype(f32), MAIN, 1)).astype(bf16)
             if s in SENT:
-                for c, (near, far) in enumerate(((phi_far, phi_hbm), (plo_far, plo_hbm))):
-                    copy = pltpu.make_async_copy(near.at[:, rows], far.at[:, rows], sems.at[c, block, SENT.index(s)])
-                    copy.start()
-                    copies.append(copy)
+                copy = pltpu.make_async_copy(
+                    far_ref.at[:, rows], far_hbm.at[:, rows], sems.at[block, SENT.index(s)]
+                )
+                copy.start()
+                copies.append(copy)
     for copy in copies:
         copy.wait()
 
 
 def degree_kernel(
     t_ref,
-    phi_ref,
-    plo_ref,
-    phi_hbm,
-    plo_hbm,
+    near_ref,
+    far_hbm,
     tab_ref,
     resp_ref,
     o_ref,
-    phi_far,
-    plo_far,
+    far_ref,
     sum_ref,
     fold_ref,
     rest_ref,
@@ -289,8 +299,9 @@
     copies = []
     for s in SENT:
         rows = pl.ds(SLOT_BASE[s], DEGREES[s])
-        for c, (far, near) in enumerate(((phi_hbm, phi_far), (plo_hbm, plo_far))):
-            copies.append(pltpu.make_async_copy(far.at[:, rows], near.at[:, rows], sems.at[c, SENT.index(s)]))
+        copies.append(
+            pltpu.make_async_copy(far_hbm.at[:, rows], far_ref.at[:, rows], sems.at[SENT.index(s)])
+        )
     for copy in copies:
         copy.start()
     device = lax.axis_index("lon") * LAT + lax.axis_index("lat")
@@ -319,16 +330,19 @@
                 spread = jnp.where(own, mains[c][p][SLOTS : SLOTS + 1], 0.0)
                 group = 2 * y + c
                 rest_ref[pl.ds(16 * p, 16), LANES * group : LANES * (group + 1)] = spread
+    spreader = ones_where(iota((LANES, LANES), 0) % REST == iota((LANES, LANES), 1) % REST)
     lane_in = iota((LAT * LANES, LANES), 0)
     lane_out = iota((LAT * LANES, LANES), 1)
     place = ones_where(
-        jnp.logical_and(lane_in % REST == lane_out % REST, lane_in // LANES == lane_out // REST)
+        jnp.logical_and(lane_in % REST == lane_out % REST, lane_in // LANES == lane_out // REST % LAT)
     )
     rest_hi, rest_lo = split(rest_ref[...])
     rest = dot(rest_hi, place) + dot(rest_lo, place)
     fold_ref[:, DEPTH - LANES :] = rest * tab_ref[3, pl.ds(HALF, 1), :]
     fold_hi, fold_lo = split(fold_ref[...])
-    both = jnp.concatenate([fold_hi, fold_lo], axis=0)
+    below = iota((32, DEPTH), 1) < DEPTH - MAIN
+    both = jnp.concatenate([fold_hi, jnp.where(below, fold_lo, jnp.zeros_like(fold_lo))], axis=0)
+    main_hi = fold_hi[:, : DEPTH - LANES]
     back_ref[...] = jnp.zeros(back_ref.shape, f32)
     tables = [None] * SLOTS
     spectra = [None] * SLOTS
@@ -337,12 +351,12 @@
             for copy in copies:
                 copy.wait()
         rows = pl.ds(SLOT_BASE[s], DEGREES[s])
-        hi_ref, lo_ref = (phi_ref, plo_ref) if s in KEPT else (phi_far, plo_far)
-        phi = jnp.concatenate([hi_ref[b, rows, :] for b in range(HALF + 1)], axis=1)
-        plo = jnp.concatenate([lo_ref[b, rows, :] for b in range(HALF + 1)], axis=1)
+        ref = near_ref if s in KEPT else far_ref
+        phi = jnp.concatenate([ref[b, rows, :] for b in (*range(HALF), 2 * HALF)], axis=1)
+        plo = jnp.concatenate([ref[HALF + b, rows, :] for b in range(HALF)], axis=1)
         tables[s] = phi, plo
         main = dot_nt(both, phi)
-        spectra[s] = main[:32] + (main[32:] + dot_nt(fold_hi, plo))
+        spectra[s] = main[:32] + (main[32:] + dot_nt(main_hi, plo))
     for s in range(SLOTS):
         count = DEGREES[s]
         phi, plo = tables[s]
@@ -365,17 +379,18 @@
         )
         hi, lo = split(four)
         out = dot(jnp.concatenate([hi, lo], axis=0), phi)
-        sums = out[:8] + (out[8:] + dot(hi, plo))
+        both_rest = out[:8, DEPTH - LANES :]
+        lower = jnp.concatenate([dot(hi, plo), pltpu.roll(both_rest, MAIN, 1)], axis=1)
+        sums = out[:8] + (out[8:] + lower)
         for c in range(2):
             back_ref[pl.ds(8 * c + s, 1), :] = sums[c : c + 1] + sums[2 + c : 3 + c]
             back_ref[pl.ds(16 + 8 * c + s, 1), :] = sums[c : c + 1] - sums[2 + c : 3 + c]
-    pick_in = iota((LANES, LAT * LANES), 0)
-    pick_out = iota((LANES, LAT * LANES), 1)
-    pick = ones_where(
-        jnp.logical_and(pick_in % REST == pick_out % REST, pick_in // REST == pick_out // LANES)
+    packed = back_ref[:, DEPTH - LANES :]
+    group = iota((32, LANES), 1) // REST
+    rest_hi, rest_lo = split(
+        jnp.concatenate([jnp.where(group == g, packed, 0.0) for g in range(LAT)], axis=0)
     )
-    rest_hi, rest_lo = split(back_ref[:, DEPTH - LANES :])
-    rest = dot(rest_hi, pick) + dot(rest_lo, pick)
+    rest = dot(rest_hi, spreader) + dot(rest_lo, spreader)
     for p in range(2):
         for y in range(HALF):
             band = y if p == 0 else LAT - 1 - y
@@ -388,8 +403,8 @@
                     sum_ref[pl.ds(row, ROWS), :] = jnp.where(first, real, pltpu.roll(imag, MAIN, 1))
                 else:
                     sum_ref[pl.ds(row, ROWS), :] = jnp.where(first, pltpu.roll(real, MAIN, 1), imag)
-                group = 2 * y + c
-                kept = jnp.where(own, rest[16 * p : 16 * (p + 1), LANES * group : LANES * (group + 1)], 0.0)
+                row_of = 32 * (2 * y + c) + 16 * p
+                kept = jnp.where(own, rest[row_of : row_of + 16], 0.0)
                 sum_ref[pl.ds(row + SLOTS, 1), :] = jnp.sum(kept, axis=0, keepdims=True)
     for c in range(2):
         total = sum_ref[pl.ds(block * c, block), :]
@@ -397,8 +412,7 @@
             o_ref[pl.ds(block * (2 * i + c), block), :] = total
 
 
-def half_inverse(ref, whi_ref, wlo_ref):
-    cos, sin = phases(lax.axis_index("lon"))
+def half_inverse(ref, cos, sin, whi_ref, wlo_ref):
     lane = iota((DEVICES, LANES), 1)
     is_main = lane < MAIN
     is_rest = lane // REST == MAIN // REST
@@ -413,15 +427,27 @@
             body = pltpu.roll(main, MAIN, 1) if c else main
             parts.append(jnp.where(is_main, body, jnp.where(is_rest, moved, 0.0)))
         real, imag = parts
-        hi, lo = split(jnp.concatenate([real * cos - imag * sin, real * sin + imag * cos], axis=0))
+        pair = jnp.concatenate(split(jnp.concatenate([real * cos - imag * sin, real * sin + imag * cos], axis=0)), axis=1)
         whi = whi_ref[:, 256 * s : 256 * (s + 1)]
         wlo = wlo_ref[:, 256 * s : 256 * (s + 1)]
-        terms = dot(whi, hi) + (dot(wlo, hi) + dot(whi, lo))
+        terms = dot(whi, pair) + dot(wlo, pair)
         total = terms if total is None else total + terms
-    return total
-
-
-def own_inverse_kernel(r_ref, base_ref, turn_ref, o_ref, whi_ref, wlo_ref):
+    return total[:, :LANES] + total[:, LANES:]
+
+
+def placed(heights, owner):
+    part = (lax.axis_index("lon") & 1) ^ owner
+    north = lax.axis_index("lat") < HALF
+    row = iota((BAND, LANES), 0)
+    place = jnp.where(north, row, BAND - 1 - row) - PART * part
+    inside = jnp.logical_and(place >= 0, place < PART)
+    order = ones_where(jnp.logical_and(iota((BAND, LANES), 1) == place, inside))
+    first = heights.astype(bf16)
+    second, third = split(heights - first.astype(f32))
+    return dot_nt(order, first) + (dot_nt(order, second) + dot_nt(order, third))
+
+
+def own_inverse_kernel(r_ref, base_ref, turn_ref, o_ref, phase_ref, whi_ref, wlo_ref):
     base_cos = base_ref[:, :DEVICES]
     base_sin = base_ref[:, DEVICES:]
     for s in range(SLOTS):
@@ -435,21 +461,15 @@
         whi, wlo = split(jnp.concatenate(wave, axis=1))
         whi_ref[:, 256 * s : 256 * (s + 1)] = whi
         wlo_ref[:, 256 * s : 256 * (s + 1)] = wlo
-    o_ref[...] = half_inverse(r_ref, whi_ref, wlo_ref)
-
-
-def inverse_kernel(g_ref, own_ref, whi_ref, wlo_ref, o_ref):
-    part = lax.axis_index("lon") & 1
-    north = lax.axis_index("lat") < HALF
-    total = jnp.concatenate([own_ref[...], half_inverse(g_ref, whi_ref, wlo_ref)], axis=1)
-    row = iota((BAND, 2 * LANES), 0)
-    place = jnp.where(north, row, BAND - 1 - row) - PART * part
-    mine = jnp.logical_and(place >= 0, place < PART)
-    other = jnp.where(place < 0, place + PART, place - PART) + LANES
-    order = ones_where(iota((BAND, 2 * LANES), 1) == jnp.where(mine, place, other))
-    first, rest_of = split(total)
-    second, third = split(total - first.astype(f32))
-    o_ref[0] = dot_nt(order, first) + (dot_nt(order, second) + dot_nt(order, third))
+    cos, sin = phases(lax.axis_index("lon"))
+    phase_ref[0] = cos
+    phase_ref[1] = sin
+    o_ref[...] = placed(half_inverse(r_ref, cos, sin, whi_ref, wlo_ref), 0)
+
+
+def inverse_kernel(g_ref, own_ref, phase_ref, whi_ref, wlo_ref, o_ref):
+    heights = half_inverse(g_ref, phase_ref[0], phase_ref[1], whi_ref, wlo_ref)
+    o_ref[0] = own_ref[...] + placed(heights, 1)
 
 
 def vmem(n):
@@ -496,29 +516,36 @@
     tables = jnp.asarray(row_tables())
     packed = jax.ShapeDtypeStruct((DEVICES * ROWS, LANES), f32)
     got = swapped(height)
-    kept = jax.ShapeDtypeStruct((HALF + 1, KEPT_ROWS, LANES), bf16)
-    sent = pltpu.HBM((HALF + 1, SENT_ROWS, LANES), bf16)
-    far = [pltpu.VMEM((HALF + 1, SENT_ROWS, LANES), bf16)] * 2
-    near_hi, near_lo, far_hi, far_lo = pl.pallas_call(
+    kept = jax.ShapeDtypeStruct((2 * HALF + 1, KEPT_ROWS, LANES), bf16)
+    sent = pltpu.HBM((2 * HALF + 1, SENT_ROWS, LANES), bf16)
+    far = [pltpu.VMEM((2 * HALF + 1, SENT_ROWS, LANES), bf16)]
+    near_legendre, far_legendre = pl.pallas_call(
         legendre_kernel,
-        out_shape=(kept, kept, sent, sent),
+        out_shape=(kept, sent),
         in_specs=[pl.BlockSpec(memory_space=pltpu.SMEM)] + vmem(1),
-        out_specs=tuple(vmem(2) + hbm(2)),
+        out_specs=tuple(vmem(1) + hbm(1)),
         scratch_shapes=far
         + [
             pltpu.VMEM((SLOTS * DEVICES * 8, LANES), f32),
-            pltpu.SemaphoreType.DMA((2, SLOTS, len(SENT))),
+            pltpu.SemaphoreType.DMA((SLOTS, len(SENT))),
         ],
         compiler_params=limit(16),
         name="legendre",
     )(recurrence_factors(device), tables)
     operand = jax.ShapeDtypeStruct((LANES, CELLS), bf16)
     waves = jax.ShapeDtypeStruct((2 * MODES, CELLS), bf16)
-    own_hi, own_lo, whi, wlo = pl.pallas_call(
+    own_half = pl.pallas_call(
         own_kernel,
-        out_shape=(operand, operand, waves, waves),
+        out_shape=(
+            operand,
+            operand,
+            waves,
+            waves,
+            jax.ShapeDtypeStruct((4, 16, LANES), f32),
+            jax.ShapeDtypeStruct((LANES, BAND), bf16),
+        ),
         in_specs=hbm(2),
-        out_specs=tuple(vmem(4)),
+        out_specs=tuple(vmem(6)),
         scratch_shapes=[
             pltpu.VMEM((1, BAND, CELLS), f32),
             pltpu.VMEM((2 * DEVICES + 16, CELLS), f32),
@@ -530,16 +557,16 @@
     shares = pl.pallas_call(
         forward_kernel,
         out_shape=packed,
-        in_specs=vmem(5),
+        in_specs=vmem(7),
         out_specs=vmem(1)[0],
         compiler_params=limit(12),
         name="forward_dft",
-    )(got, own_hi, own_lo, whi, wlo)
+    )(got, *own_half)
     arrived = exchanged(shares)
     synthesis = pl.pallas_call(
         degree_kernel,
         out_shape=packed,
-        in_specs=vmem(3) + hbm(2) + vmem(2),
+        in_specs=vmem(2) + hbm(1) + vmem(2),
         out_specs=vmem(1)[0],
         scratch_shapes=far
         + [
@@ -547,31 +574,36 @@
             pltpu.VMEM((32, DEPTH), f32),
             pltpu.VMEM((32, LAT * LANES), f32),
             pltpu.VMEM((32, DEPTH), f32),
-            pltpu.SemaphoreType.DMA((2, len(SENT))),
+            pltpu.SemaphoreType.DMA((len(SENT),)),
         ],
         compiler_params=limit(16),
         name="degrees",
-    )(arrived, near_hi, near_lo, in_hbm(far_hi), in_hbm(far_lo), tables, response.reshape(1, MODES))
+    )(arrived, near_legendre, in_hbm(far_legendre), tables, response.reshape(1, MODES))
     returned = exchanged(synthesis)
     other = swapped(returned)
     waves = jax.ShapeDtypeStruct((CELLS, 2 * MODES), bf16)
     base, turns = last_waves(table)
-    own, thi, tlo = pl.pallas_call(
+    own, phase, thi, tlo = pl.pallas_call(
         own_inverse_kernel,
-        out_shape=(jax.ShapeDtypeStruct((CELLS, LANES), f32), waves, waves),
+        out_shape=(
+            jax.ShapeDtypeStruct((BAND, CELLS), f32),
+            jax.ShapeDtypeStruct((2, DEVICES, LANES), f32),
+            waves,
+            waves,
+        ),
         in_specs=vmem(3),
-        out_specs=tuple(vmem(3)),
+        out_specs=tuple(vmem(4)),
         compiler_params=limit(12),
         name="own_inverse_dft",
     )(returned, jnp.asarray(base), jnp.asarray(turns))
     return pl.pallas_call(
         inverse_kernel,
         out_shape=jax.ShapeDtypeStruct((1, BAND, CELLS), f32),
-        in_specs=vmem(4),
+        in_specs=vmem(5),
         out_specs=vmem(1)[0],
         compiler_params=limit(12),
         name="inverse_dft",
-    )(other, own, thi, tlo)
+    )(other, own, phase, thi, tlo)
 
 
 def solution(mesh):

time: 51.2 us -> 50.6 us (0.988)
  Pallas kernels: 14.4 us -> 13.8 us
    pallas_call x5, Pallas kernels: 12.7 us -> 12.2 us  [the longest x1 5.01 us: shards(): pl.pallas_call(legendre_kernel, out_shape=(kept, sent), in_specs=[pl.Bloc...]
where the time goes in v4:
time: 50.6 us; the launch traced here: 50.4 us
  blocking collectives  16.5 us (33%)
  Pallas kernels  13.8 us (27%)
  starting transfers between devices  13.2 us (26%)
  waiting for transfers between devices  6.71 us (13%)
    all_to_all x1, blocking collectives, exchanged(): lax.all_to_all(x, ('lon', 'lat'), split_axis=0, concat_axis=0, tiled=True)  16.5 us
    all_to_all x1, starting transfers between devices, exchanged(): lax.all_to_all(x, ('lon', 'lat'), split_axis=0, concat_axis=0, tiled=True)  10.2 us
    all_to_all x1, waiting for transfers between devices, exchanged(): lax.all_to_all(x, ('lon', 'lat'), split_axis=0, concat_axis=0, tiled=True)  6.38 us
    pallas_call x1, Pallas kernels, shards(): pl.pallas_call(legendre_kernel, out_shape=(kept, sent), in_specs=[pl.Bloc...  5.01 us
    pallas_call x1, Pallas kernels, shards(): pl.pallas_call(degree_kernel, out_shape=packed, in_specs=vmem(2) + hbm(1)...  3.05 us
    ppermute x2, starting transfers between devices, swapped(): return lax.ppermute(x, 'lon', [(i, i ^ 1) for i in range(LON)])  2.96 us
    pallas_call x1, Pallas kernels, shards(): pl.pallas_call(forward_kernel, out_shape=packed, in_specs=vmem(7), out_sp...  1.71 us
    pallas_call x1, Pallas kernels, shards(): pl.pallas_call(inverse_kernel, out_shape=jax.ShapeDtypeStruct((1, BAND, C...  1.57 us
  transfers between devices with their start and end apart: 3, of which 2 were waited for; matrix products, arithmetic and copies ran while one was open for 0% of the time, Pallas kernels for 15%

profile of v4, /device:TPU:1, one launch (start us, length us, event | category | flops | bytes accessed | tf_op | source)
XLA Modules:
  0.0 50.4 jit_solution(9874391647555700791)
XLA Ops:
  0.0 0.0 copy-start.2
  0.0 0.0 copy-start.3
  0.0 1.4 %collective-permute-start = (f32[1,144,256]{2,1,0:T(8,128)}, f32[1,144,256]{2,1,0:T(8,128)S(1)}, u32[]{:S(2)}, u32[]{:S(2)}) collective-permute-start(f32[1,144,256]{2,1,0:T(8,128)} %h_hbm.1), channel_id=1, source_target_pairs={{0,8},{8,0},{16,24},{24,16},{32,40},{40,32},{48,56},{56,48},{64,72... | collective-permute-start | bytes 442376 | tf_op jit(solution)/shard_map/ppermute | solution.py:492
  1.4 1.4 %own_half.1 = (bf16[128,256]{1,0:T(8,128)(2,1)S(1)}, bf16[128,256]{1,0:T(8,128)(2,1)S(1)}, bf16[1280,256]{1,0:T(8,128)(2,1)S(1)}, bf16[1280,256]{1,0:T(8,128)(2,...) custom-call(f32[1,144,256]{2,1,0:T(8,128)} %h_hbm.1, f32[272,256]{1,0:T(8,128)} %constant.33.clone.wave_hbm), custom_call_target="tpu_custom_call" | custom-call | tf_op jit(solution)/shard_map/own_half/pallas_call | solution.py:537
  2.9 0.0 collective-permute-done.g_ref
  2.9 1.7 %forward_dft.1 = f32[768,128]{1,0:T(8,128)} custom-call(f32[1,144,256]{2,1,0:T(8,128)S(1)} %collective-permute-done.g_ref, bf16[128,256]{1,0:T(8,128)(2,1)S(1)} %get-tuple-element.17.own_hi_ref, bf16[128,256]{1,0:T(8,128)(2,1)S(1)} %get-tuple-element.18.own_lo_ref, bf16[1280,256]{1,0:T(8,128)(2,1)S(1)} %get-tuple-element.19.whi_ref, ...), custom_call_target="tpu_custom_call" | custom-call | tf_op jit(solution)/shard_map/forward_dft/pallas_call | solution.py:557
  4.6 10.2 %all-to-all-start = ((f32[128,1,768]{2,1,0:T(1,128)}), f32[128,1,768]{2,1,0:T(1,128)S(1)}, u32[]{:S(2)}, u32[]{:S(2)}) async-start(f32[128,1,768]{2,1,0:T(1,128)} %bitcast), calls=%async_computation | async-start | bytes 786432 | tf_op jit(solution)/shard_map/all_to_all | solution.py:497
  14.8 0.0 copy-done.3
  14.8 0.1 sqrt_select_fusion
  15.0 0.0 copy-done.2
  15.0 5.0 %legendre.1 = (bf16[9,1152,128]{2,1,0:T(8,128)(2,1)S(1)}, bf16[9,768,128]{2,1,0:T(8,128)(2,1)}) custom-call(f32[6400]{0:T(1024)S(1)} %reshape.324.coef_ref, f32[5,8,128]{2,1,0:T(8,128)S(1)} %copy-done.2), custom_call_target="tpu_custom_call" | custom-call | tf_op jit(solution)/shard_map/legendre/pallas_call | solution.py:522
  20.0 6.4 %all-to-all-done = f32[128,1,768]{2,1,0:T(1,128)S(1)} async-done(((f32[128,1,768]{2,1,0:T(1,128)}), f32[128,1,768]{2,1,0:T(1,128)S(1)}, u32[]{:S(2)}, u32[]{:S(2)}) %all-to-all-start) | async-done | bytes 393248 | tf_op jit(solution)/shard_map/all_to_all | solution.py:497
  26.4 0.0 copy-start
  26.4 0.0 copy-start.1
  26.4 3.1 %degrees.1 = f32[768,128]{1,0:T(8,128)S(1)} custom-call(f32[768,128]{1,0:T(8,128)S(1)} %bitcast.4, bf16[9,1152,128]{2,1,0:T(8,128)(2,1)S(1)} %get-tuple-element.23.near_ref, bf16[9,768,128]{2,1,0:T(8,128)(2,1)} %get-tuple-element.24.far_hbm, f32[5,8,128]{2,1,0:T(8,128)S(1)} %copy-done.2, f32[1,640]{1,0:T(1,128)S(1)} %reshape.325.resp_ref), custom_call_target="tpu_custom_call" | custom-call | tf_op jit(solution)/shard_map/degrees/pallas_call | solution.py:566
  29.4 16.5 %all_to_all.10 = f32[128,1,768]{2,1,0:T(1,128)S(1)} all-to-all(f32[128,1,768]{2,1,0:T(1,128)S(1)} %bitcast.7), channel_id=1, replica_groups=mesh['lon'=16,'lat'=8] {'lon','lat'}, dimensions={0} | all-to-all | bytes 786432 | tf_op jit(solution)/shard_map/all_to_all | solution.py:497
  45.9 1.6 %collective-permute-start.1 = (f32[768,128]{1,0:T(8,128)S(1)}, f32[768,128]{1,0:T(8,128)S(1)}, u32[]{:S(2)}, u32[]{:S(2)}) collective-permute-start(f32[768,128]{1,0:T(8,128)S(1)} %bitcast.5), channel_id=1, source_target_pairs={{0,8},{8,0},{16,24},{24,16},{32,40},{40,32},{48,56},{56,48},{64,72... | collective-permute-start | bytes 1179656 | tf_op jit(solution)/shard_map/ppermute | solution.py:492
  47.5 0.0 copy-done
  47.5 0.0 copy-done.1
  47.5 1.0 %own_inverse_dft.1 = (f32[144,256]{1,0:T(8,128)S(1)}, f32[2,128,128]{2,1,0:T(8,128)S(1)}, bf16[256,1280]{1,0:T(8,128)(2,1)S(1)}, bf16[256,1280]{1,0:T(8,128)(2,1)S(1)}) custom-call(f32[768,128]{1,0:T(8,128)S(1)} %bitcast.6, f32[256,256]{1,0:T(8,128)S(1)} %copy-done, f32[320,128]{1,0:T(8,128)S(1)} %copy-done.1), custom_call_target="tpu_custom_call" | custom-call | tf_op jit(solution)/shard_map/own_inverse_dft/pallas_call | solution.py:586
  48.5 0.3 collective-permute-done.1.g_ref
  48.8 1.6 %inverse_dft.1 = f32[1,144,256]{2,1,0:T(8,128)} custom-call(f32[768,128]{1,0:T(8,128)S(1)} %collective-permute-done.1.g_ref, f32[144,256]{1,0:T(8,128)S(1)} %get-tuple-element.25.own_ref, f32[2,128,128]{2,1,0:T(8,128)S(1)} %get-tuple-element.26.phase_ref, bf16[256,1280]{1,0:T(8,128)(2,1)S(1)} %get-tuple-element.27.whi_ref, ...), custom_call_target="tpu_custom_call" | custom-call | tf_op jit(solution)/shard_map/inverse_dft/pallas_call | solution.py:599
  (7 shorter events, 0.0 us)
Async XLA Ops:
  0.0 15.0 %copy-start.2 = (f32[5,8,128]{2,1,0:T(8,128)S(1)}, f32[5,8,128]{2,1,0:T(8,128)}, u32[]{:S(2)}) copy-start(f32[5,8,128]{2,1,0:T(8,128)} %constant.32.clone.tab_ref) | copy-start | bytes 61444
  0.0 14.8 %copy-start.3 = (f32[640]{0:T(1024)S(1)}, f32[640]{0:T(1024)}, u32[]{:S(2)}) copy-start(f32[640]{0:T(1024)} %param.7) | copy-start | bytes 7684
  0.0 2.9 %collective-permute-start = (f32[1,144,256]{2,1,0:T(8,128)}, f32[1,144,256]{2,1,0:T(8,128)S(1)}, u32[]{:S(2)}, u32[]{:S(2)}) collective-permute-start(f32[1,144,256]{2,1,0:T(8,128)} %h_hbm.1), channel_id=1, source_target_pairs={{0,8},{8,0},{16,24},{24,16},{32,40},{40,32},{48,56},{56,48},{64,72... | collective-permute-start | bytes 442376 | tf_op jit(solution)/shard_map/ppermute | solution.py:492
  4.6 21.8 %all-to-all-start = ((f32[128,1,768]{2,1,0:T(1,128)}), f32[128,1,768]{2,1,0:T(1,128)S(1)}, u32[]{:S(2)}, u32[]{:S(2)}) async-start(f32[128,1,768]{2,1,0:T(1,128)} %bitcast), calls=%async_computation | async-start | bytes 786432 | tf_op jit(solution)/shard_map/all_to_all | solution.py:497
  26.4 21.1 %copy-start = (f32[256,256]{1,0:T(8,128)S(1)}, f32[256,256]{1,0:T(8,128)}, u32[]{:S(2)}) copy-start(f32[256,256]{1,0:T(8,128)} %constant.34.clone.base_ref) | copy-start | bytes 786436
  26.4 21.1 %copy-start.1 = (f32[320,128]{1,0:T(8,128)S(1)}, f32[320,128]{1,0:T(8,128)}, u32[]{:S(2)}) copy-start(f32[320,128]{1,0:T(8,128)} %constant.35.clone.turn_ref) | copy-start | bytes 491524
  45.9 2.9 %collective-permute-start.1 = (f32[768,128]{1,0:T(8,128)S(1)}, f32[768,128]{1,0:T(8,128)S(1)}, u32[]{:S(2)}, u32[]{:S(2)}) collective-permute-start(f32[768,128]{1,0:T(8,128)S(1)} %bitcast.5), channel_id=1, source_target_pairs={{0,8},{8,0},{16,24},{24,16},{32,40},{40,32},{48,56},{56,48},{64,72... | collective-permute-start | bytes 1179656 | tf_op jit(solution)/shard_map/ppermute | solution.py:492

commit v5 on v4

--- a/solution.py
+++ b/solution.py
@@ -435,13 +435,10 @@
     return total[:, :LANES] + total[:, LANES:]
 
 
-def placed(heights, owner):
-    part = (lax.axis_index("lon") & 1) ^ owner
+def in_rows(heights):
     north = lax.axis_index("lat") < HALF
-    row = iota((BAND, LANES), 0)
-    place = jnp.where(north, row, BAND - 1 - row) - PART * part
-    inside = jnp.logical_and(place >= 0, place < PART)
-    order = ones_where(jnp.logical_and(iota((BAND, LANES), 1) == place, inside))
+    row = iota((PART, LANES), 0)
+    order = ones_where(iota((PART, LANES), 1) == jnp.where(north, row, PART - 1 - row))
     first = heights.astype(bf16)
     second, third = split(heights - first.astype(f32))
     return dot_nt(order, first) + (dot_nt(order, second) + dot_nt(order, third))
@@ -464,12 +461,21 @@
     cos, sin = phases(lax.axis_index("lon"))
     phase_ref[0] = cos
     phase_ref[1] = sin
-    o_ref[...] = placed(half_inverse(r_ref, cos, sin, whi_ref, wlo_ref), 0)
-
-
-def inverse_kernel(g_ref, own_ref, phase_ref, whi_ref, wlo_ref, o_ref):
-    heights = half_inverse(g_ref, phase_ref[0], phase_ref[1], whi_ref, wlo_ref)
-    o_ref[0] = own_ref[...] + placed(heights, 1)
+    o_ref[...] = in_rows(half_inverse(r_ref, cos, sin, whi_ref, wlo_ref))
+
+
+def inverse_kernel(g_ref, own_ref, phase_ref, whi_ref, wlo_ref, o_hbm, got_ref, sems):
+    part = lax.axis_index("lon") & 1
+    north = lax.axis_index("lat") < HALF
+    own_first = pl.multiple_of(PART * jnp.where(north, part, 1 - part), 8)
+    got_first = pl.multiple_of(PART * jnp.where(north, 1 - part, part), 8)
+    own_copy = pltpu.make_async_copy(own_ref, o_hbm.at[0, pl.ds(own_first, PART)], sems.at[0])
+    got_copy = pltpu.make_async_copy(got_ref, o_hbm.at[0, pl.ds(got_first, PART)], sems.at[1])
+    own_copy.start()
+    got_ref[...] = in_rows(half_inverse(g_ref, phase_ref[0], phase_ref[1], whi_ref, wlo_ref))
+    got_copy.start()
+    own_copy.wait()
+    got_copy.wait()
 
 
 def vmem(n):
@@ -586,7 +592,7 @@
     own, phase, thi, tlo = pl.pallas_call(
         own_inverse_kernel,
         out_shape=(
-            jax.ShapeDtypeStruct((BAND, CELLS), f32),
+            jax.ShapeDtypeStruct((PART, CELLS), f32),
             jax.ShapeDtypeStruct((2, DEVICES, LANES), f32),
             waves,
             waves,
@@ -600,7 +606,8 @@
         inverse_kernel,
         out_shape=jax.ShapeDtypeStruct((1, BAND, CELLS), f32),
         in_specs=vmem(5),
-        out_specs=vmem(1)[0],
+        out_specs=hbm(1)[0],
+        scratch_shapes=[pltpu.VMEM((PART, CELLS), f32), pltpu.SemaphoreType.DMA((2,))],
         compiler_params=limit(12),
         name="inverse_dft",
     )(other, own, phase, thi, tlo)

time: 50.6 us -> 50.6 us (level)
  no operation moved by 1% of the time
where the time goes in v5:
time: 50.6 us; the launch traced here: 50.3 us
  blocking collectives  16.5 us (33%)
  Pallas kernels  13.7 us (27%)
  starting transfers between devices  13.2 us (26%)
  waiting for transfers between devices  6.79 us (13%)
    all_to_all x1, blocking collectives, exchanged(): lax.all_to_all(x, ('lon', 'lat'), split_axis=0, concat_axis=0, tiled=True)  16.5 us
    all_to_all x1, starting transfers between devices, exchanged(): lax.all_to_all(x, ('lon', 'lat'), split_axis=0, concat_axis=0, tiled=True)  10.2 us
    all_to_all x1, waiting for transfers between devices, exchanged(): lax.all_to_all(x, ('lon', 'lat'), split_axis=0, concat_axis=0, tiled=True)  6.38 us
    pallas_call x1, Pallas kernels, shards(): pl.pallas_call(legendre_kernel, out_shape=(kept, sent), in_specs=[pl.Bloc...  5.01 us
    pallas_call x1, Pallas kernels, shards(): pl.pallas_call(degree_kernel, out_shape=packed, in_specs=vmem(2) + hbm(1)...  3.05 us
    ppermute x2, starting transfers between devices, swapped(): return lax.ppermute(x, 'lon', [(i, i ^ 1) for i in range(LON)])  2.96 us
    pallas_call x1, Pallas kernels, shards(): pl.pallas_call(forward_kernel, out_shape=packed, in_specs=vmem(7), out_sp...  1.71 us
    pallas_call x1, Pallas kernels, shards(): pl.pallas_call(inverse_kernel, out_shape=jax.ShapeDtypeStruct((1, BAND, C...  1.52 us
  transfers between devices with their start and end apart: 3, of which 2 were waited for; matrix products, arithmetic and copies ran while one was open for 0% of the time, Pallas kernels for 15%

profile of v5, /device:TPU:1, one launch (start us, length us, event | category | flops | bytes accessed | tf_op | source)
XLA Modules:
  0.0 50.3 jit_solution(10168232988950953811)
XLA Ops:
  0.0 0.0 copy-start.2
  0.0 0.0 copy-start.3
  0.0 1.4 %collective-permute-start = (f32[1,144,256]{2,1,0:T(8,128)}, f32[1,144,256]{2,1,0:T(8,128)S(1)}, u32[]{:S(2)}, u32[]{:S(2)}) collective-permute-start(f32[1,144,256]{2,1,0:T(8,128)} %h_hbm.1), channel_id=1, source_target_pairs={{0,8},{8,0},{16,24},{24,16},{32,40},{40,32},{48,56},{56,48},{64,72... | collective-permute-start | bytes 442376 | tf_op jit(solution)/shard_map/ppermute | solution.py:498
  1.4 1.4 %own_half.1 = (bf16[128,256]{1,0:T(8,128)(2,1)S(1)}, bf16[128,256]{1,0:T(8,128)(2,1)S(1)}, bf16[1280,256]{1,0:T(8,128)(2,1)S(1)}, bf16[1280,256]{1,0:T(8,128)(2,...) custom-call(f32[1,144,256]{2,1,0:T(8,128)} %h_hbm.1, f32[272,256]{1,0:T(8,128)} %constant.33.clone.wave_hbm), custom_call_target="tpu_custom_call" | custom-call | tf_op jit(solution)/shard_map/own_half/pallas_call | solution.py:543
  2.9 0.0 collective-permute-done.g_ref
  2.9 1.7 %forward_dft.1 = f32[768,128]{1,0:T(8,128)} custom-call(f32[1,144,256]{2,1,0:T(8,128)S(1)} %collective-permute-done.g_ref, bf16[128,256]{1,0:T(8,128)(2,1)S(1)} %get-tuple-element.17.own_hi_ref, bf16[128,256]{1,0:T(8,128)(2,1)S(1)} %get-tuple-element.18.own_lo_ref, bf16[1280,256]{1,0:T(8,128)(2,1)S(1)} %get-tuple-element.19.whi_ref, ...), custom_call_target="tpu_custom_call" | custom-call | tf_op jit(solution)/shard_map/forward_dft/pallas_call | solution.py:563
  4.6 10.2 %all-to-all-start = ((f32[128,1,768]{2,1,0:T(1,128)}), f32[128,1,768]{2,1,0:T(1,128)S(1)}, u32[]{:S(2)}, u32[]{:S(2)}) async-start(f32[128,1,768]{2,1,0:T(1,128)} %bitcast), calls=%async_computation | async-start | bytes 786432 | tf_op jit(solution)/shard_map/all_to_all | solution.py:503
  14.8 0.0 copy-done.3
  14.8 0.1 sqrt_select_fusion
  15.0 0.0 copy-done.2
  15.0 5.0 %legendre.1 = (bf16[9,1152,128]{2,1,0:T(8,128)(2,1)S(1)}, bf16[9,768,128]{2,1,0:T(8,128)(2,1)}) custom-call(f32[6400]{0:T(1024)S(1)} %reshape.324.coef_ref, f32[5,8,128]{2,1,0:T(8,128)S(1)} %copy-done.2), custom_call_target="tpu_custom_call" | custom-call | tf_op jit(solution)/shard_map/legendre/pallas_call | solution.py:528
  20.0 6.4 %all-to-all-done = f32[128,1,768]{2,1,0:T(1,128)S(1)} async-done(((f32[128,1,768]{2,1,0:T(1,128)}), f32[128,1,768]{2,1,0:T(1,128)S(1)}, u32[]{:S(2)}, u32[]{:S(2)}) %all-to-all-start) | async-done | bytes 393248 | tf_op jit(solution)/shard_map/all_to_all | solution.py:503
  26.4 0.0 copy-start
  26.4 0.0 copy-start.1
  26.4 3.1 %degrees.1 = f32[768,128]{1,0:T(8,128)S(1)} custom-call(f32[768,128]{1,0:T(8,128)S(1)} %bitcast.4, bf16[9,1152,128]{2,1,0:T(8,128)(2,1)S(1)} %get-tuple-element.23.near_ref, bf16[9,768,128]{2,1,0:T(8,128)(2,1)} %get-tuple-element.24.far_hbm, f32[5,8,128]{2,1,0:T(8,128)S(1)} %copy-done.2, f32[1,640]{1,0:T(1,128)S(1)} %reshape.325.resp_ref), custom_call_target="tpu_custom_call" | custom-call | tf_op jit(solution)/shard_map/degrees/pallas_call | solution.py:572
  29.4 16.5 %all_to_all.10 = f32[128,1,768]{2,1,0:T(1,128)S(1)} all-to-all(f32[128,1,768]{2,1,0:T(1,128)S(1)} %bitcast.7), channel_id=1, replica_groups=mesh['lon'=16,'lat'=8] {'lon','lat'}, dimensions={0} | all-to-all | bytes 786432 | tf_op jit(solution)/shard_map/all_to_all | solution.py:503
  45.9 1.6 %collective-permute-start.1 = (f32[768,128]{1,0:T(8,128)S(1)}, f32[768,128]{1,0:T(8,128)S(1)}, u32[]{:S(2)}, u32[]{:S(2)}) collective-permute-start(f32[768,128]{1,0:T(8,128)S(1)} %bitcast.5), channel_id=1, source_target_pairs={{0,8},{8,0},{16,24},{24,16},{32,40},{40,32},{48,56},{56,48},{64,72... | collective-permute-start | bytes 1179656 | tf_op jit(solution)/shard_map/ppermute | solution.py:498
  47.5 0.0 copy-done
  47.5 0.0 copy-done.1
  47.5 0.9 %own_inverse_dft.1 = (f32[72,256]{1,0:T(8,128)S(1)}, f32[2,128,128]{2,1,0:T(8,128)S(1)}, bf16[256,1280]{1,0:T(8,128)(2,1)S(1)}, bf16[256,1280]{1,0:T(8,128)(2,1)S(1)}) custom-call(f32[768,128]{1,0:T(8,128)S(1)} %bitcast.6, f32[256,256]{1,0:T(8,128)S(1)} %copy-done, f32[320,128]{1,0:T(8,128)S(1)} %copy-done.1), custom_call_target="tpu_custom_call" | custom-call | tf_op jit(solution)/shard_map/own_inverse_dft/pallas_call | solution.py:592
  48.4 0.4 collective-permute-done.1.g_ref
  48.8 1.5 %inverse_dft.1 = f32[1,144,256]{2,1,0:T(8,128)} custom-call(f32[768,128]{1,0:T(8,128)S(1)} %collective-permute-done.1.g_ref, f32[72,256]{1,0:T(8,128)S(1)} %get-tuple-element.25.own_ref, f32[2,128,128]{2,1,0:T(8,128)S(1)} %get-tuple-element.26.phase_ref, bf16[256,1280]{1,0:T(8,128)(2,1)S(1)} %get-tuple-element.27.whi_ref, ...), custom_call_target="tpu_custom_call" | custom-call | tf_op jit(solution)/shard_map/inverse_dft/pallas_call | solution.py:605
  (7 shorter events, 0.0 us)
Async XLA Ops:
  0.0 15.0 %copy-start.2 = (f32[5,8,128]{2,1,0:T(8,128)S(1)}, f32[5,8,128]{2,1,0:T(8,128)}, u32[]{:S(2)}) copy-start(f32[5,8,128]{2,1,0:T(8,128)} %constant.32.clone.tab_ref) | copy-start | bytes 61444
  0.0 14.8 %copy-start.3 = (f32[640]{0:T(1024)S(1)}, f32[640]{0:T(1024)}, u32[]{:S(2)}) copy-start(f32[640]{0:T(1024)} %param.7) | copy-start | bytes 7684
  0.0 2.9 %collective-permute-start = (f32[1,144,256]{2,1,0:T(8,128)}, f32[1,144,256]{2,1,0:T(8,128)S(1)}, u32[]{:S(2)}, u32[]{:S(2)}) collective-permute-start(f32[1,144,256]{2,1,0:T(8,128)} %h_hbm.1), channel_id=1, source_target_pairs={{0,8},{8,0},{16,24},{24,16},{32,40},{40,32},{48,56},{56,48},{64,72... | collective-permute-start | bytes 442376 | tf_op jit(solution)/shard_map/ppermute | solution.py:498
  4.6 21.8 %all-to-all-start = ((f32[128,1,768]{2,1,0:T(1,128)}), f32[128,1,768]{2,1,0:T(1,128)S(1)}, u32[]{:S(2)}, u32[]{:S(2)}) async-start(f32[128,1,768]{2,1,0:T(1,128)} %bitcast), calls=%async_computation | async-start | bytes 786432 | tf_op jit(solution)/shard_map/all_to_all | solution.py:503
  26.4 21.1 %copy-start = (f32[256,256]{1,0:T(8,128)S(1)}, f32[256,256]{1,0:T(8,128)}, u32[]{:S(2)}) copy-start(f32[256,256]{1,0:T(8,128)} %constant.34.clone.base_ref) | copy-start | bytes 786436
  26.4 21.1 %copy-start.1 = (f32[320,128]{1,0:T(8,128)S(1)}, f32[320,128]{1,0:T(8,128)}, u32[]{:S(2)}) copy-start(f32[320,128]{1,0:T(8,128)} %constant.35.clone.turn_ref) | copy-start | bytes 491524
  45.9 2.9 %collective-permute-start.1 = (f32[768,128]{1,0:T(8,128)S(1)}, f32[768,128]{1,0:T(8,128)S(1)}, u32[]{:S(2)}, u32[]{:S(2)}) collective-permute-start(f32[768,128]{1,0:T(8,128)S(1)} %bitcast.5), channel_id=1, source_target_pairs={{0,8},{8,0},{16,24},{24,16},{32,40},{40,32},{48,56},{56,48},{64,72... | collective-permute-start | bytes 1179656 | tf_op jit(solution)/shard_map/ppermute | solution.py:498
